TPU v7x, 256 devices: a whole 4x4x8 slice. The times are simulated.
256 devices in a mesh: seq: 32 (over z, x), head: 8 (over y, core).
Axes of the slice: x: 4, y: 4, z: 8, core: 2. Of those that a mesh axis runs over, the one named last changes fastest.
Arguments:
- queries: bfloat16 [16384, 4096], P('seq', 'head'), may hold values from -80 to 80
- new_keys: bfloat16 [16384, 1024], P('seq', 'head'), may hold values from -8 to 8
- new_values: bfloat16 [16384, 1024], P('seq', 'head'), may hold values from -6 to 6
Outputs:
- attended: bfloat16 [16384, 4096], P('seq', 'head')
- key_low: float32 [128, 1024], P('seq', 'head')
- key_step: float32 [128, 1024], P('seq', 'head')
- value_low: float32 [16384], P('seq')
- value_step: float32 [16384], P('seq')
All inputs are finite; a program needn't handle non-finite values.
Results may differ from a plain program's by a relative error of at most 0.0045.
Values may be sent and summed in bfloat16 or wider, within the bound.
A program may use at most 64 MiB of HBM per device.

v0:
```python
import math

import jax
import jax.numpy as jnp
from jax import lax
from jax.sharding import PartitionSpec as P

HEADS = 32
KV_HEADS = 8
HEAD_DIM = 128
WINDOW = 4096
GROUP = 128


negative_fill = -1e30


def passed_along(block, axis, distance):
    devices = range(lax.axis_size(axis))
    route = [(i - distance, i) for i in devices if i - distance in devices]
    return lax.ppermute(block, axis, route)


def copy_for_each(array, axis):
    copies = jnp.broadcast_to(array, (lax.axis_size(axis), *array.shape))
    return lax.all_to_all(copies, axis, split_axis=0, concat_axis=0, tiled=True)


def taken_together(array, axis):
    everything = copy_for_each(array, axis)
    return jnp.max(everything, axis=0)


def taken_together_2(array, axis):
    everything = copy_for_each(array, axis)
    return jnp.min(everything, axis=0)


def shards(queries, new_keys, new_values):
    tok_rows = new_keys.shape[0]
    kv_width = new_keys.shape[1]
    kv_local = kv_width // HEAD_DIM
    group_size = HEADS // KV_HEADS
    halo_count = WINDOW // tok_rows
    scale = 1.0 / math.sqrt(HEAD_DIM)
    stacked = jnp.stack((new_keys, new_values), 0)
    context = stacked
    held = 1
    while held < halo_count + 1:
        needed = min(held, halo_count + 1 - held)
        tail_part = context[:, (held - needed) * tok_rows :]
        arrived = passed_along(tail_part, "seq", held)
        context = jnp.concatenate((arrived, context), 1)
        held = held + needed
    total_keys = (halo_count + 1) * tok_rows
    query_size = 512
    key_size = 512
    query_count = tok_rows // query_size
    key_count = total_keys // key_size
    base_pos = lax.axis_index("seq") * tok_rows
    query_heads = queries.reshape(tok_rows, kv_local, group_size, HEAD_DIM)

    def query_step(query_index):
        query_pos = base_pos + query_index * query_size + jnp.arange(query_size, dtype=jnp.int32)

        def key_step(key_index, carry):
            running_max, running_total, running_acc = carry
            key_block = lax.dynamic_slice_in_dim(context, key_index * key_size, key_size, 1)
            key_part = key_block[0].reshape(key_size, kv_local, HEAD_DIM)
            value_part = key_block[1].reshape(key_size, kv_local, HEAD_DIM)
            key_pos = (
                base_pos
                - halo_count * tok_rows
                + key_index * key_size
                + jnp.arange(key_size, dtype=jnp.int32)
            )
            valid = (
                (key_pos[None, :] <= query_pos[:, None])
                & (key_pos[None, :] > query_pos[:, None] - WINDOW)
                & (key_pos[None, :] >= 0)
            )
            scores = (
                jnp.einsum(
                    "qhgd,khd->hgqk", query_heads, key_part, preferred_element_type=jnp.float32
                )
                * scale
            )
            masked = jnp.where(valid[None, None], scores, negative_fill)
            new_max = jnp.maximum(running_max, jnp.max(masked, axis=-1))
            weights = jnp.where(valid[None, None], jnp.exp(masked - new_max[..., None]), 0.0)
            rescale = jnp.exp(running_max - new_max)
            new_total = running_total * rescale + jnp.sum(weights, axis=-1)
            product = jnp.einsum(
                "hgqk,khd->hgqd",
                weights.astype(jnp.bfloat16),
                value_part,
                preferred_element_type=jnp.float32,
            )
            new_acc = running_acc * rescale[..., None] + product
            return (new_max, new_total, new_acc)

        start_max = jnp.full((kv_local, group_size, query_size), negative_fill, jnp.float32)
        start_total = jnp.zeros((kv_local, group_size, query_size), jnp.float32)
        start_acc = jnp.zeros((kv_local, group_size, query_size, HEAD_DIM), jnp.float32)
        final_max, final_total, final_acc = lax.fori_loop(
            0, key_count, key_step, (start_max, start_total, start_acc)
        )
        result = (final_acc / final_total[..., None]).astype(jnp.bfloat16)
        return jnp.transpose(result, (2, 0, 1, 3)).reshape(
            query_size, kv_local * group_size * HEAD_DIM
        )

    attended = lax.map(query_step, jnp.arange(query_count, dtype=jnp.int32)).reshape(
        tok_rows, kv_local * group_size * HEAD_DIM
    )
    grouped = new_keys.astype(jnp.float32).reshape(tok_rows // GROUP, GROUP, kv_width)
    key_low = jnp.min(grouped, axis=1)
    key_step_out = (jnp.max(grouped, axis=1) - key_low) / 3.0
    value_rows = new_values.astype(jnp.float32)
    local_top = jnp.max(value_rows, axis=1)
    local_bottom = jnp.min(value_rows, axis=1)
    row_top = taken_together(local_top, "head")
    row_bottom = taken_together_2(local_bottom, "head")
    value_step_out = (row_top - row_bottom) / 3.0
    return (attended, key_low, key_step_out, row_bottom, value_step_out)


def solution(mesh):
    return jax.shard_map(
        shards,
        mesh=mesh,
        in_specs=(P("seq", "head"), P("seq", "head"), P("seq", "head")),
        out_specs=(P("seq", "head"), P("seq", "head"), P("seq", "head"), P("seq"), P("seq")),
        check_vma=False,
    )
```

profile of v0, /device:TPU:160, one launch (start us, length us, event | category | flops | bytes accessed | tf_op | source)
XLA Modules:
  0.0 166.2 jit_solution(4180931028703118539)
XLA Ops:
  0.7 1.1 pad_maximum_fusion
  1.7 3.4 %collective-permute-start.1 = (bf16[2,512,128]{2,1,0:T(8,128)(2,1)S(1)}, bf16[2,512,128]{2,1,0:T(8,128)(2,1)S(1)}, u32[]{:S(2)}, u32[]{:S(2)}) collective-permute-start(bf16[2,512,128]{2,1,0:T(8,128)(2,1)S(1)} %pad_maximum_fusion), channel_id=1, source_target_pairs={{0,8},{8,16},{16,24},{24,32},{32,40},{40,48},{48,56},{56,64},{64,7... | collective-permute-start | bytes 786440 | tf_op jit(solution)/shard_map/ppermute | solution.py:21
  5.1 8.6 %collective-permute-done.1 = bf16[2,512,128]{2,1,0:T(8,128)(2,1)S(1)} collective-permute-done((bf16[2,512,128]{2,1,0:T(8,128)(2,1)S(1)}, bf16[2,512,128]{2,1,0:T(8,128)(2,1)S(1)}, u32[]{:S(2)}, u32[]{:S(2)}) %collective-permute-start.1) | collective-permute-done | bytes 262176 | tf_op jit(solution)/shard_map/ppermute | solution.py:21
  13.8 1.0 maximum_maximum_fusion.1
  14.8 2.8 %collective-permute-start.2 = (bf16[2,1024,128]{2,1,0:T(8,128)(2,1)S(1)}, bf16[2,1024,128]{2,1,0:T(8,128)(2,1)S(1)}, u32[]{:S(2)}, u32[]{:S(2)}) collective-permute-start(bf16[2,1024,128]{2,1,0:T(8,128)(2,1)S(1)} %maximum_maximum_fusion.1), channel_id=1, source_target_pairs={{0,16},{8,24},{16,32},{24,40},{32,48},{40,56},{48,64},{56,72},{64,... | collective-permute-start | bytes 1572872 | tf_op jit(solution)/shard_map/ppermute | solution.py:21
  17.6 14.3 %collective-permute-done.2 = bf16[2,1024,128]{2,1,0:T(8,128)(2,1)S(1)} collective-permute-done((bf16[2,1024,128]{2,1,0:T(8,128)(2,1)S(1)}, bf16[2,1024,128]{2,1,0:T(8,128)(2,1)S(1)}, u32[]{:S(2)}, u32[]{:S(2)}) %collective-permute-start.2) | collective-permute-done | bytes 524320 | tf_op jit(solution)/shard_map/ppermute | solution.py:21
  31.9 2.0 %maximum_maximum_fusion = bf16[2,2048,128]{2,1,0:T(8,128)(2,1)} fusion(bf16[1,512,128]{2,1,0:T(8,128)(2,1)} %bitcast.92, bf16[1,512,128]{2,1,0:T(8,128)(2,1)} %bitcast.96, bf16[2,512,128]{2,1,0:T(8,128)(2,1)S(1)} %collective-permute-done.1, bf16[2,1024,128]{2,1,0:T(8,128)(2,1)S(1)} %collective-permute-done.2), kind=kLoop, calls=%fused_computation.31 | loop fusion | flops 4194304 | bytes 2097152 | tf_op jit(solution)/shard_map/concatenate | solution.py:53
  33.9 2.9 %collective-permute-start.3 = (bf16[2,2048,128]{2,1,0:T(8,128)(2,1)}, bf16[2,2048,128]{2,1,0:T(8,128)(2,1)}, u32[]{:S(2)}, u32[]{:S(2)}) collective-permute-start(bf16[2,2048,128]{2,1,0:T(8,128)(2,1)} %maximum_maximum_fusion), channel_id=1, source_target_pairs={{0,32},{8,40},{16,48},{24,56},{32,64},{40,72},{48,80},{56,88},{64,... | collective-permute-start | bytes 3145736 | tf_op jit(solution)/shard_map/ppermute | solution.py:21
  36.8 1.9 %collective-permute-start = (bf16[2,512,128]{2,1,0:T(8,128)(2,1)S(1)}, bf16[2,512,128]{2,1,0:T(8,128)(2,1)}, u32[]{:S(2)}, u32[]{:S(2)}) collective-permute-start(bf16[2,512,128]{2,1,0:T(8,128)(2,1)S(1)} %pad_maximum_fusion), channel_id=1, source_target_pairs={{0,64},{8,72},{16,80},{24,88},{32,96},{40,104},{48,112},{56,120},{... | collective-permute-start | bytes 786440 | tf_op jit(solution)/shard_map/ppermute | solution.py:21
  38.9 0.6 broadcast_in_dim.77
  39.5 4.5 %all-to-all-start = ((f32[8,1,512]{2,1,0:T(1,128)}), f32[8,1,512]{2,1,0:T(1,128)S(1)}, u32[]{:S(2)}, u32[]{:S(2)}) async-start(f32[8,1,512]{2,1,0:T(1,128)} %broadcast_in_dim.77), calls=%async_computation | async-start | bytes 32768 | tf_op jit(solution)/shard_map/all_to_all | solution.py:26
  44.1 0.1 reduce_max.46
  44.2 5.1 %all-to-all-done = f32[8,1,512]{2,1,0:T(1,128)S(1)} async-done(((f32[8,1,512]{2,1,0:T(1,128)}), f32[8,1,512]{2,1,0:T(1,128)S(1)}, u32[]{:S(2)}, u32[]{:S(2)}) %all-to-all-start) | async-done | bytes 16416 | tf_op jit(solution)/shard_map/all_to_all | solution.py:26
  49.4 0.6 broadcast_in_dim.78
  50.0 3.3 %all-to-all-start.1 = ((f32[8,1,512]{2,1,0:T(1,128)}), f32[8,1,512]{2,1,0:T(1,128)S(1)}, u32[]{:S(2)}, u32[]{:S(2)}) async-start(f32[8,1,512]{2,1,0:T(1,128)} %broadcast_in_dim.78), calls=%async_computation.1 | async-start | bytes 32768 | tf_op jit(solution)/shard_map/all_to_all | solution.py:26
  53.3 0.6 fusion.24
  53.9 0.2 copy.19
  54.1 0.3 copy.20
  54.4 4.1 %all-to-all-done.1 = f32[8,1,512]{2,1,0:T(1,128)S(1)} async-done(((f32[8,1,512]{2,1,0:T(1,128)}), f32[8,1,512]{2,1,0:T(1,128)S(1)}, u32[]{:S(2)}, u32[]{:S(2)}) %all-to-all-start.1) | async-done | bytes 16416 | tf_op jit(solution)/shard_map/all_to_all | solution.py:26
  58.6 0.6 subtract_multiply_fusion
  59.2 15.4 %collective-permute-done = bf16[2,512,128]{2,1,0:T(8,128)(2,1)} collective-permute-done((bf16[2,512,128]{2,1,0:T(8,128)(2,1)S(1)}, bf16[2,512,128]{2,1,0:T(8,128)(2,1)}, u32[]{:S(2)}, u32[]{:S(2)}) %collective-permute-start) | collective-permute-done | bytes 262176 | tf_op jit(solution)/shard_map/ppermute | solution.py:21
  74.6 1.0 constant_dynamic-update-slice_fusion.4
  75.6 1.4 constant_dynamic-update-slice_fusion.3
  77.2 1.4 copy-done.4
  78.6 86.0 %while.29 = (s32[]{:T(128)}, f32[1,4,512]{2,1,0:T(4,128)S(1)}, f32[1,4,512]{2,1,0:T(4,128)S(1)}, f32[1,4,512,128]{3,2,1,0:T(8,128)S(1)}, s32[]{:T(128)}, /*index...) while((s32[]{:T(128)}, f32[1,4,512]{2,1,0:T(4,128)S(1)}, ...), condition=%wide.region_3.0_spmd.clone, body=%wide.region_0.3_spmd.clone.sunk | while | flops 552352256 | bytes 33436928 | solution.py:105
  78.6 0.3 and_and_fusion.2
  78.9 3.7 %fusion.31 = (f32[4,512]{1,0:T(4,128)S(1)}, f32[512,512,4]{1,0,2:T(8,128)}) fusion(pred[512,512]{0,1:T(8,128)(4,1)S(1)} %and_and_fusion.2, bf16[512,1,4,128]{3,0,2,1:T(8,128)(2,1)S(1)} %get-tuple-element.426, bf16[2,4608,128]{2,1,0:T(8,128)(2,1)} %get-tuple-element.425, s32[]{:T(128)S(6)} %select_n.76), kind=kOutput, calls=%fused_computation.3.clone.1 | convolution fusion | flops 271579136 | bytes 5120004 | tf_op jit(solution)/shard_map/while/body/eval_jaxpr/while/body/eval_jaxpr/qhgd,khd->hgqk/dot_general | solution.py:83
  82.6 4.3 %fusion.34 = f32[1,4,512,128]{3,2,1,0:T(8,128)S(1)} fusion(f32[512,512,4]{1,0,2:T(8,128)} %get-tuple-element.392, f32[4,512]{1,0:T(4,128)S(1)} %bitcast.98, pred[512,512]{0,1:T(8,128)(4,1)S(1)} %and_and_fusion.2, f32[1,4,512,128]{3,2,1,0:T(8,128)S(1)} %get-tuple-element.410, f32[4,512]{1,0:T(4,128)S(1)} %get-tuple-element.393, pred[]{:T(512)S(6)} %compare.3, ...), kind=kOutput, calls=%fused_computation.10.clone.1 | convolution fusion | flops 274464768 | bytes 6701065 | tf_op jit(solution)/shard_map/while/body/eval_jaxpr/while/body/eval_jaxpr/hgqk,khd->hgqd/dot_general | solution.py:93
  87.0 1.1 fusion.33
  88.2 0.3 and_and_fusion.2
  88.5 3.7 %fusion.31 = (f32[4,512]{1,0:T(4,128)S(1)}, f32[512,512,4]{1,0,2:T(8,128)}) fusion(pred[512,512]{0,1:T(8,128)(4,1)S(1)} %and_and_fusion.2, bf16[512,1,4,128]{3,0,2,1:T(8,128)(2,1)S(1)} %get-tuple-element.426, bf16[2,4608,128]{2,1,0:T(8,128)(2,1)} %get-tuple-element.425, s32[]{:T(128)S(6)} %select_n.76), kind=kOutput, calls=%fused_computation.3.clone.1 | convolution fusion | flops 271579136 | bytes 5120004 | tf_op jit(solution)/shard_map/while/body/eval_jaxpr/while/body/eval_jaxpr/qhgd,khd->hgqk/dot_general | solution.py:83
  92.2 4.3 %fusion.34 = f32[1,4,512,128]{3,2,1,0:T(8,128)S(1)} fusion(f32[512,512,4]{1,0,2:T(8,128)} %get-tuple-element.392, f32[4,512]{1,0:T(4,128)S(1)} %bitcast.98, pred[512,512]{0,1:T(8,128)(4,1)S(1)} %and_and_fusion.2, f32[1,4,512,128]{3,2,1,0:T(8,128)S(1)} %get-tuple-element.410, f32[4,512]{1,0:T(4,128)S(1)} %get-tuple-element.393, pred[]{:T(512)S(6)} %compare.3, ...), kind=kOutput, calls=%fused_computation.10.clone.1 | convolution fusion | flops 274464768 | bytes 6701065 | tf_op jit(solution)/shard_map/while/body/eval_jaxpr/while/body/eval_jaxpr/hgqk,khd->hgqd/dot_general | solution.py:93
  96.6 1.1 fusion.33
  97.7 0.3 and_and_fusion.2
  98.0 3.7 %fusion.31 = (f32[4,512]{1,0:T(4,128)S(1)}, f32[512,512,4]{1,0,2:T(8,128)}) fusion(pred[512,512]{0,1:T(8,128)(4,1)S(1)} %and_and_fusion.2, bf16[512,1,4,128]{3,0,2,1:T(8,128)(2,1)S(1)} %get-tuple-element.426, bf16[2,4608,128]{2,1,0:T(8,128)(2,1)} %get-tuple-element.425, s32[]{:T(128)S(6)} %select_n.76), kind=kOutput, calls=%fused_computation.3.clone.1 | convolution fusion | flops 271579136 | bytes 5120004 | tf_op jit(solution)/shard_map/while/body/eval_jaxpr/while/body/eval_jaxpr/qhgd,khd->hgqk/dot_general | solution.py:83
  101.8 4.3 %fusion.34 = f32[1,4,512,128]{3,2,1,0:T(8,128)S(1)} fusion(f32[512,512,4]{1,0,2:T(8,128)} %get-tuple-element.392, f32[4,512]{1,0:T(4,128)S(1)} %bitcast.98, pred[512,512]{0,1:T(8,128)(4,1)S(1)} %and_and_fusion.2, f32[1,4,512,128]{3,2,1,0:T(8,128)S(1)} %get-tuple-element.410, f32[4,512]{1,0:T(4,128)S(1)} %get-tuple-element.393, pred[]{:T(512)S(6)} %compare.3, ...), kind=kOutput, calls=%fused_computation.10.clone.1 | convolution fusion | flops 274464768 | bytes 6701065 | tf_op jit(solution)/shard_map/while/body/eval_jaxpr/while/body/eval_jaxpr/hgqk,khd->hgqd/dot_general | solution.py:93
  106.1 1.1 fusion.33
  107.3 0.3 and_and_fusion.2
  107.6 3.7 %fusion.31 = (f32[4,512]{1,0:T(4,128)S(1)}, f32[512,512,4]{1,0,2:T(8,128)}) fusion(pred[512,512]{0,1:T(8,128)(4,1)S(1)} %and_and_fusion.2, bf16[512,1,4,128]{3,0,2,1:T(8,128)(2,1)S(1)} %get-tuple-element.426, bf16[2,4608,128]{2,1,0:T(8,128)(2,1)} %get-tuple-element.425, s32[]{:T(128)S(6)} %select_n.76), kind=kOutput, calls=%fused_computation.3.clone.1 | convolution fusion | flops 271579136 | bytes 5120004 | tf_op jit(solution)/shard_map/while/body/eval_jaxpr/while/body/eval_jaxpr/qhgd,khd->hgqk/dot_general | solution.py:83
  111.3 4.3 %fusion.34 = f32[1,4,512,128]{3,2,1,0:T(8,128)S(1)} fusion(f32[512,512,4]{1,0,2:T(8,128)} %get-tuple-element.392, f32[4,512]{1,0:T(4,128)S(1)} %bitcast.98, pred[512,512]{0,1:T(8,128)(4,1)S(1)} %and_and_fusion.2, f32[1,4,512,128]{3,2,1,0:T(8,128)S(1)} %get-tuple-element.410, f32[4,512]{1,0:T(4,128)S(1)} %get-tuple-element.393, pred[]{:T(512)S(6)} %compare.3, ...), kind=kOutput, calls=%fused_computation.10.clone.1 | convolution fusion | flops 274464768 | bytes 6701065 | tf_op jit(solution)/shard_map/while/body/eval_jaxpr/while/body/eval_jaxpr/hgqk,khd->hgqd/dot_general | solution.py:93
  115.7 1.1 fusion.33
  116.8 0.3 and_and_fusion.2
  117.2 3.7 %fusion.31 = (f32[4,512]{1,0:T(4,128)S(1)}, f32[512,512,4]{1,0,2:T(8,128)}) fusion(pred[512,512]{0,1:T(8,128)(4,1)S(1)} %and_and_fusion.2, bf16[512,1,4,128]{3,0,2,1:T(8,128)(2,1)S(1)} %get-tuple-element.426, bf16[2,4608,128]{2,1,0:T(8,128)(2,1)} %get-tuple-element.425, s32[]{:T(128)S(6)} %select_n.76), kind=kOutput, calls=%fused_computation.3.clone.1 | convolution fusion | flops 271579136 | bytes 5120004 | tf_op jit(solution)/shard_map/while/body/eval_jaxpr/while/body/eval_jaxpr/qhgd,khd->hgqk/dot_general | solution.py:83
  120.9 4.3 %fusion.34 = f32[1,4,512,128]{3,2,1,0:T(8,128)S(1)} fusion(f32[512,512,4]{1,0,2:T(8,128)} %get-tuple-element.392, f32[4,512]{1,0:T(4,128)S(1)} %bitcast.98, pred[512,512]{0,1:T(8,128)(4,1)S(1)} %and_and_fusion.2, f32[1,4,512,128]{3,2,1,0:T(8,128)S(1)} %get-tuple-element.410, f32[4,512]{1,0:T(4,128)S(1)} %get-tuple-element.393, pred[]{:T(512)S(6)} %compare.3, ...), kind=kOutput, calls=%fused_computation.10.clone.1 | convolution fusion | flops 274464768 | bytes 6701065 | tf_op jit(solution)/shard_map/while/body/eval_jaxpr/while/body/eval_jaxpr/hgqk,khd->hgqd/dot_general | solution.py:93
  125.2 1.1 fusion.33
  126.4 0.3 and_and_fusion.2
  126.7 3.7 %fusion.31 = (f32[4,512]{1,0:T(4,128)S(1)}, f32[512,512,4]{1,0,2:T(8,128)}) fusion(pred[512,512]{0,1:T(8,128)(4,1)S(1)} %and_and_fusion.2, bf16[512,1,4,128]{3,0,2,1:T(8,128)(2,1)S(1)} %get-tuple-element.426, bf16[2,4608,128]{2,1,0:T(8,128)(2,1)} %get-tuple-element.425, s32[]{:T(128)S(6)} %select_n.76), kind=kOutput, calls=%fused_computation.3.clone.1 | convolution fusion | flops 271579136 | bytes 5120004 | tf_op jit(solution)/shard_map/while/body/eval_jaxpr/while/body/eval_jaxpr/qhgd,khd->hgqk/dot_general | solution.py:83
  130.4 4.3 %fusion.34 = f32[1,4,512,128]{3,2,1,0:T(8,128)S(1)} fusion(f32[512,512,4]{1,0,2:T(8,128)} %get-tuple-element.392, f32[4,512]{1,0:T(4,128)S(1)} %bitcast.98, pred[512,512]{0,1:T(8,128)(4,1)S(1)} %and_and_fusion.2, f32[1,4,512,128]{3,2,1,0:T(8,128)S(1)} %get-tuple-element.410, f32[4,512]{1,0:T(4,128)S(1)} %get-tuple-element.393, pred[]{:T(512)S(6)} %compare.3, ...), kind=kOutput, calls=%fused_computation.10.clone.1 | convolution fusion | flops 274464768 | bytes 6701065 | tf_op jit(solution)/shard_map/while/body/eval_jaxpr/while/body/eval_jaxpr/hgqk,khd->hgqd/dot_general | solution.py:93
  134.8 1.1 fusion.33
  135.9 0.3 and_and_fusion.2
  136.3 3.7 %fusion.31 = (f32[4,512]{1,0:T(4,128)S(1)}, f32[512,512,4]{1,0,2:T(8,128)}) fusion(pred[512,512]{0,1:T(8,128)(4,1)S(1)} %and_and_fusion.2, bf16[512,1,4,128]{3,0,2,1:T(8,128)(2,1)S(1)} %get-tuple-element.426, bf16[2,4608,128]{2,1,0:T(8,128)(2,1)} %get-tuple-element.425, s32[]{:T(128)S(6)} %select_n.76), kind=kOutput, calls=%fused_computation.3.clone.1 | convolution fusion | flops 271579136 | bytes 5120004 | tf_op jit(solution)/shard_map/while/body/eval_jaxpr/while/body/eval_jaxpr/qhgd,khd->hgqk/dot_general | solution.py:83
  140.0 4.3 %fusion.34 = f32[1,4,512,128]{3,2,1,0:T(8,128)S(1)} fusion(f32[512,512,4]{1,0,2:T(8,128)} %get-tuple-element.392, f32[4,512]{1,0:T(4,128)S(1)} %bitcast.98, pred[512,512]{0,1:T(8,128)(4,1)S(1)} %and_and_fusion.2, f32[1,4,512,128]{3,2,1,0:T(8,128)S(1)} %get-tuple-element.410, f32[4,512]{1,0:T(4,128)S(1)} %get-tuple-element.393, pred[]{:T(512)S(6)} %compare.3, ...), kind=kOutput, calls=%fused_computation.10.clone.1 | convolution fusion | flops 274464768 | bytes 6701065 | tf_op jit(solution)/shard_map/while/body/eval_jaxpr/while/body/eval_jaxpr/hgqk,khd->hgqd/dot_general | solution.py:93
  144.3 1.1 fusion.33
  145.5 0.3 and_and_fusion.2
  145.8 3.7 %fusion.31 = (f32[4,512]{1,0:T(4,128)S(1)}, f32[512,512,4]{1,0,2:T(8,128)}) fusion(pred[512,512]{0,1:T(8,128)(4,1)S(1)} %and_and_fusion.2, bf16[512,1,4,128]{3,0,2,1:T(8,128)(2,1)S(1)} %get-tuple-element.426, bf16[2,4608,128]{2,1,0:T(8,128)(2,1)} %get-tuple-element.425, s32[]{:T(128)S(6)} %select_n.76), kind=kOutput, calls=%fused_computation.3.clone.1 | convolution fusion | flops 271579136 | bytes 5120004 | tf_op jit(solution)/shard_map/while/body/eval_jaxpr/while/body/eval_jaxpr/qhgd,khd->hgqk/dot_general | solution.py:83
  149.6 4.3 %fusion.34 = f32[1,4,512,128]{3,2,1,0:T(8,128)S(1)} fusion(f32[512,512,4]{1,0,2:T(8,128)} %get-tuple-element.392, f32[4,512]{1,0:T(4,128)S(1)} %bitcast.98, pred[512,512]{0,1:T(8,128)(4,1)S(1)} %and_and_fusion.2, f32[1,4,512,128]{3,2,1,0:T(8,128)S(1)} %get-tuple-element.410, f32[4,512]{1,0:T(4,128)S(1)} %get-tuple-element.393, pred[]{:T(512)S(6)} %compare.3, ...), kind=kOutput, calls=%fused_computation.10.clone.1 | convolution fusion | flops 274464768 | bytes 6701065 | tf_op jit(solution)/shard_map/while/body/eval_jaxpr/while/body/eval_jaxpr/hgqk,khd->hgqd/dot_general | solution.py:93
  153.9 1.1 fusion.33
  155.1 0.3 and_and_fusion.2
  155.4 3.7 %fusion.31 = (f32[4,512]{1,0:T(4,128)S(1)}, f32[512,512,4]{1,0,2:T(8,128)}) fusion(pred[512,512]{0,1:T(8,128)(4,1)S(1)} %and_and_fusion.2, bf16[512,1,4,128]{3,0,2,1:T(8,128)(2,1)S(1)} %get-tuple-element.426, bf16[2,4608,128]{2,1,0:T(8,128)(2,1)} %get-tuple-element.425, s32[]{:T(128)S(6)} %select_n.76), kind=kOutput, calls=%fused_computation.3.clone.1 | convolution fusion | flops 271579136 | bytes 5120004 | tf_op jit(solution)/shard_map/while/body/eval_jaxpr/while/body/eval_jaxpr/qhgd,khd->hgqk/dot_general | solution.py:83
  159.1 4.3 %fusion.34 = f32[1,4,512,128]{3,2,1,0:T(8,128)S(1)} fusion(f32[512,512,4]{1,0,2:T(8,128)} %get-tuple-element.392, f32[4,512]{1,0:T(4,128)S(1)} %bitcast.98, pred[512,512]{0,1:T(8,128)(4,1)S(1)} %and_and_fusion.2, f32[1,4,512,128]{3,2,1,0:T(8,128)S(1)} %get-tuple-element.410, f32[4,512]{1,0:T(4,128)S(1)} %get-tuple-element.393, pred[]{:T(512)S(6)} %compare.3, ...), kind=kOutput, calls=%fused_computation.10.clone.1 | convolution fusion | flops 274464768 | bytes 6701065 | tf_op jit(solution)/shard_map/while/body/eval_jaxpr/while/body/eval_jaxpr/hgqk,khd->hgqd/dot_general | solution.py:93
  163.5 1.1 fusion.33
  164.6 0.3 fusion.23
  164.9 0.4 copy.21
  165.3 0.9 copy.29
  (95 shorter events, 0.9 us)
Async XLA Ops:
  0.6 43.4 %copy-start.2 = (bf16[512,128]{1,0:T(8,128)(2,1)S(1)}, bf16[512,128]{1,0:T(8,128)(2,1)}, u32[]{:S(2)}) copy-start(bf16[512,128]{1,0:T(8,128)(2,1)} %param.6) | copy-start | bytes 393220
  0.6 38.1 %copy-start.1 = (bf16[512,128]{1,0:T(8,128)(2,1)S(1)}, bf16[512,128]{1,0:T(8,128)(2,1)}, u32[]{:S(2)}) copy-start(bf16[512,128]{1,0:T(8,128)(2,1)} %param.7) | copy-start | bytes 393220
  0.7 53.2 %copy-start.3 = (bf16[512,512]{1,0:T(8,128)(2,1)S(1)}, bf16[512,512]{1,0:T(8,128)(2,1)}, u32[]{:S(2)}) copy-start(bf16[512,512]{1,0:T(8,128)(2,1)} %param.5) | copy-start | bytes 1572868
  1.7 12.0 %collective-permute-start.1 = (bf16[2,512,128]{2,1,0:T(8,128)(2,1)S(1)}, bf16[2,512,128]{2,1,0:T(8,128)(2,1)S(1)}, u32[]{:S(2)}, u32[]{:S(2)}) collective-permute-start(bf16[2,512,128]{2,1,0:T(8,128)(2,1)S(1)} %pad_maximum_fusion), channel_id=1, source_target_pairs={{0,8},{8,16},{16,24},{24,32},{32,40},{40,48},{48,56},{56,64},{64,7... | collective-permute-start | bytes 786440 | tf_op jit(solution)/shard_map/ppermute | solution.py:21
  14.8 17.1 %collective-permute-start.2 = (bf16[2,1024,128]{2,1,0:T(8,128)(2,1)S(1)}, bf16[2,1024,128]{2,1,0:T(8,128)(2,1)S(1)}, u32[]{:S(2)}, u32[]{:S(2)}) collective-permute-start(bf16[2,1024,128]{2,1,0:T(8,128)(2,1)S(1)} %maximum_maximum_fusion.1), channel_id=1, source_target_pairs={{0,16},{8,24},{16,32},{24,40},{32,48},{40,56},{48,64},{56,72},{64,... | collective-permute-start | bytes 1572872 | tf_op jit(solution)/shard_map/ppermute | solution.py:21
  33.9 41.7 %collective-permute-start.3 = (bf16[2,2048,128]{2,1,0:T(8,128)(2,1)}, bf16[2,2048,128]{2,1,0:T(8,128)(2,1)}, u32[]{:S(2)}, u32[]{:S(2)}) collective-permute-start(bf16[2,2048,128]{2,1,0:T(8,128)(2,1)} %maximum_maximum_fusion), channel_id=1, source_target_pairs={{0,32},{8,40},{16,48},{24,56},{32,64},{40,72},{48,80},{56,88},{64,... | collective-permute-start | bytes 3145736 | tf_op jit(solution)/shard_map/ppermute | solution.py:21
  36.8 37.8 %collective-permute-start = (bf16[2,512,128]{2,1,0:T(8,128)(2,1)S(1)}, bf16[2,512,128]{2,1,0:T(8,128)(2,1)}, u32[]{:S(2)}, u32[]{:S(2)}) collective-permute-start(bf16[2,512,128]{2,1,0:T(8,128)(2,1)S(1)} %pad_maximum_fusion), channel_id=1, source_target_pairs={{0,64},{8,72},{16,80},{24,88},{32,96},{40,104},{48,112},{56,120},{... | collective-permute-start | bytes 786440 | tf_op jit(solution)/shard_map/ppermute | solution.py:21
  39.5 9.8 %all-to-all-start = ((f32[8,1,512]{2,1,0:T(1,128)}), f32[8,1,512]{2,1,0:T(1,128)S(1)}, u32[]{:S(2)}, u32[]{:S(2)}) async-start(f32[8,1,512]{2,1,0:T(1,128)} %broadcast_in_dim.77), calls=%async_computation | async-start | bytes 32768 | tf_op jit(solution)/shard_map/all_to_all | solution.py:26
  44.0 32.9 %copy-start.5 = (f32[4,128]{1,0:T(4,128)}, f32[4,128]{1,0:T(4,128)S(1)}, u32[]{:S(2)}) copy-start(f32[4,128]{1,0:T(4,128)S(1)} %convert_reduce_fusion.1) | copy-start | bytes 6148
  50.0 8.6 %all-to-all-start.1 = ((f32[8,1,512]{2,1,0:T(1,128)}), f32[8,1,512]{2,1,0:T(1,128)S(1)}, u32[]{:S(2)}, u32[]{:S(2)}) async-start(f32[8,1,512]{2,1,0:T(1,128)} %broadcast_in_dim.78), calls=%async_computation.1 | async-start | bytes 32768 | tf_op jit(solution)/shard_map/all_to_all | solution.py:26
  54.4 22.7 %copy-start.6 = (f32[512]{0:T(512)}, f32[512]{0:T(512)S(1)}, u32[]{:S(2)}) copy-start(f32[512]{0:T(512)S(1)} %reduce_min.29) | copy-start | bytes 6148
  77.2 1.4 copy-start.4
  82.6 4.4 %copy-start = (f32[512,512,4]{1,0,2:T(8,128)S(1)}, f32[512,512,4]{1,0,2:T(8,128)}, u32[]{:S(2)}) copy-start(f32[512,512,4]{1,0,2:T(8,128)} %get-tuple-element.392) | copy-start | bytes 12582916 | tf_op jit(solution)/shard_map/while/body/eval_jaxpr/while
  92.2 4.4 %copy-start = (f32[512,512,4]{1,0,2:T(8,128)S(1)}, f32[512,512,4]{1,0,2:T(8,128)}, u32[]{:S(2)}) copy-start(f32[512,512,4]{1,0,2:T(8,128)} %get-tuple-element.392) | copy-start | bytes 12582916 | tf_op jit(solution)/shard_map/while/body/eval_jaxpr/while
  101.8 4.4 %copy-start = (f32[512,512,4]{1,0,2:T(8,128)S(1)}, f32[512,512,4]{1,0,2:T(8,128)}, u32[]{:S(2)}) copy-start(f32[512,512,4]{1,0,2:T(8,128)} %get-tuple-element.392) | copy-start | bytes 12582916 | tf_op jit(solution)/shard_map/while/body/eval_jaxpr/while
  111.3 4.4 %copy-start = (f32[512,512,4]{1,0,2:T(8,128)S(1)}, f32[512,512,4]{1,0,2:T(8,128)}, u32[]{:S(2)}) copy-start(f32[512,512,4]{1,0,2:T(8,128)} %get-tuple-element.392) | copy-start | bytes 12582916 | tf_op jit(solution)/shard_map/while/body/eval_jaxpr/while
  120.9 4.4 %copy-start = (f32[512,512,4]{1,0,2:T(8,128)S(1)}, f32[512,512,4]{1,0,2:T(8,128)}, u32[]{:S(2)}) copy-start(f32[512,512,4]{1,0,2:T(8,128)} %get-tuple-element.392) | copy-start | bytes 12582916 | tf_op jit(solution)/shard_map/while/body/eval_jaxpr/while
  130.4 4.4 %copy-start = (f32[512,512,4]{1,0,2:T(8,128)S(1)}, f32[512,512,4]{1,0,2:T(8,128)}, u32[]{:S(2)}) copy-start(f32[512,512,4]{1,0,2:T(8,128)} %get-tuple-element.392) | copy-start | bytes 12582916 | tf_op jit(solution)/shard_map/while/body/eval_jaxpr/while
  140.0 4.4 %copy-start = (f32[512,512,4]{1,0,2:T(8,128)S(1)}, f32[512,512,4]{1,0,2:T(8,128)}, u32[]{:S(2)}) copy-start(f32[512,512,4]{1,0,2:T(8,128)} %get-tuple-element.392) | copy-start | bytes 12582916 | tf_op jit(solution)/shard_map/while/body/eval_jaxpr/while
  149.5 4.4 %copy-start = (f32[512,512,4]{1,0,2:T(8,128)S(1)}, f32[512,512,4]{1,0,2:T(8,128)}, u32[]{:S(2)}) copy-start(f32[512,512,4]{1,0,2:T(8,128)} %get-tuple-element.392) | copy-start | bytes 12582916 | tf_op jit(solution)/shard_map/while/body/eval_jaxpr/while
  159.1 4.4 %copy-start = (f32[512,512,4]{1,0,2:T(8,128)S(1)}, f32[512,512,4]{1,0,2:T(8,128)}, u32[]{:S(2)}) copy-start(f32[512,512,4]{1,0,2:T(8,128)} %get-tuple-element.392) | copy-start | bytes 12582916 | tf_op jit(solution)/shard_map/while/body/eval_jaxpr/while
where the time goes:
time: 167 us; the launch traced here: 166 us
  matrix products  72.3 us (43%)
  waiting for transfers between devices  47.6 us (29%)
  starting transfers between devices  18.9 us (11%)
  other arithmetic  18.7 us (11%)
  local copies, waits for them, and re-layouts  6.94 us (4%)
    dot_general x9, matrix products, key_step(): jnp.einsum('hgqk,khd->hgqd', weights.astype(jnp.bfloat16), value_part, pr...  39.1 us
    ppermute x4, waiting for transfers between devices, passed_along(): return lax.ppermute(block, axis, route)  38.3 us
    dot_general x9, matrix products, key_step(): jnp.einsum('qhgd,khd->hgqk', query_heads, key_part, preferred_element_typ...  33.3 us
    ppermute x4, starting transfers between devices, passed_along(): return lax.ppermute(block, axis, route)  11.1 us
    reduce_sum x9, other arithmetic, key_step(): new_total = running_total * rescale + jnp.sum(weights, axis=-1)  9.53 us
    all_to_all x2, waiting for transfers between devices, copy_for_each(): return lax.all_to_all(copies, axis, split_axis=0, concat_axis=0, tiled=True)  9.29 us
    all_to_all x2, starting transfers between devices, copy_for_each(): return lax.all_to_all(copies, axis, split_axis=0, concat_axis=0, tiled=True)  7.81 us
    unnamed x19, local copies, waits for them, and re-layouts  5.24 us
  transfers between devices with their start and end apart: 6, of which 5 were waited for; matrix products, arithmetic and copies ran while one was open for 3% of the time, Pallas kernels for 0%

commit v1 on v0

v1 whole, which is shorter than its diff:
```python
import functools
import math

import jax
import jax.numpy as jnp
from jax import lax
from jax.experimental import pallas as pl
from jax.experimental.pallas import tpu as pltpu
from jax.sharding import PartitionSpec as P

HEADS = 32
KV_HEADS = 8
HEAD_DIM = 128
WINDOW = 4096
GROUP = 128
PER = HEADS // KV_HEADS
TOK = 512
CHUNK = 128
TILE = 256
SPAN = TOK // TILE
XS = 4
ZS = 8
OWN = 32
LOG2E = 1.4426950408889634
SCALE = LOG2E / math.sqrt(HEAD_DIM)
NEG = -1e30

STARTS = (
    ((0, 34, 24), (1, 32, 2), (2, 33, 1), (0, 32, 2), (1, 34, 16), (2, 32, 0), (0, 33, 3), (1, 33, 3), (2, 34, 6)),
    ((0, 32, 0), (2, 33, 1), (0, 34, 14), (2, 32, 0), (0, 33, 1), (2, 34, 8)),
    ((0, 33, 1), (2, 34, 4), (0, 34, 18), (2, 33, 3), (0, 32, 0), (2, 32, 2)),
    ((2, 32, 6), (2, 34, 4), (2, 35, 5)),
)
STEPS = (
    (
        ((1, ((0, 1, 5), (1, 1, 9), (2, 1, 31))), (0, ((0, 0, 4), (1, 0, 8), (2, 0, 30)))),
        ((6, ((0, 6, 20), (1, 6, 20), (2, 6, 26), (2, 35, 7))), (18, ((0, 18, 18),)), (3, ((1, 3, 15), (1, 35, 17))), (31, ()), (4, ((0, 4, 14),)), (2, ((2, 2, 8),))),
        ((30, ()), (5, ((0, 5, 15),))),
        ((10, ((1, 10, 28), (2, 10, 20), (2, 4, 14))), (26, ()), (16, ((0, 16, 28),)), (9, ()), (7, ((1, 7, 21), (0, 7, 21), (2, 7, 27), (0, 35, 25)))),
        ((13, ()), (24, ()), (8, ())),
        ((12, ((2, 12, 22),)), (11, ((1, 11, 29),))),
        (),
        ((20, ()), (15, ()), (28, ()), (14, ())),
        ((17, ()),),
        ((23, ()), (27, ()), (19, ())),
        ((21, ()),),
        ((22, ()),),
        ((25, ()),),
        (),
        ((29, ()),),
        (),
    ),
    (
        ((24, ()), (1, ((1, 1, 3), (0, 1, 7), (2, 1, 31))), (2, ()), (0, ((1, 0, 2), (0, 0, 6), (2, 0, 30), (2, 35, 9)))),
        ((3, ((0, 3, 9),)),),
        ((8, ((1, 8, 10), (0, 8, 16), (2, 8, 26), (0, 35, 15))), (10, ()), (5, ()), (31, ((1, 31, 9), (1, 10, 24))), (7, ((2, 7, 13),)), (4, ())),
        ((30, ()), (6, ())),
        ((20, ((0, 20, 28),)), (9, ((1, 9, 11), (2, 9, 27), (0, 9, 17)))),
        ((16, ((1, 16, 28),)), (18, ()), (26, ()), (11, ((2, 11, 17),))),
        ((14, ((0, 14, 22), (2, 14, 22))), (13, ((1, 13, 23),)), (12, ())),
        ((15, ()),),
        ((27, ((1, 27, 21),)), (28, ()), (19, ((2, 19, 29),)), (17, ((1, 17, 29),))),
        (),
        ((21, ()),),
        ((23, ()), (22, ())),
        ((25, ()),),
        (),
        ((29, ()),),
        (),
    ),
    (
        ((0, ((0, 0, 12),)), (4, ((1, 4, 10), (2, 4, 26), (2, 35, 5))), (14, ()), (3, ((1, 3, 7), (0, 3, 11))), (1, ())),
        ((2, ((1, 2, 6), (0, 2, 10), (2, 2, 30), (0, 1, 13))),),
        ((8, ((2, 8, 10),)), (7, ()), (26, ((1, 26, 16),)), (12, ((2, 12, 20),)), (6, ()), (5, ((1, 5, 11), (0, 5, 23), (0, 35, 19), (2, 5, 27), (0, 14, 24), (2, 3, 31)))),
        (),
        ((18, ()), (9, ())),
        ((30, ((1, 30, 12),)), (11, ()), (16, ()), (10, ())),
        ((13, ((1, 13, 19), (2, 13, 21))),),
        ((15, ((0, 15, 25),)),),
        ((20, ()), (25, ((1, 25, 23),)), (28, ()), (27, ()), (23, ()), (17, ())),
        ((31, ()), (19, ())),
        ((22, ()), (21, ())),
        (),
        ((24, ()),),
        (),
        ((29, ()),),
        (),
    ),
    (
        ((1, ()), (2, ((1, 2, 8),)), (6, ((0, 6, 18), (2, 6, 30), (1, 6, 12), (2, 33, 7))), (18, ()), (16, ((1, 16, 18),)), (4, ((0, 4, 4),)), (0, ())),
        ((3, ()),),
        ((5, ((0, 5, 5), (2, 5, 27))),),
        ((12, ((2, 12, 14),)), (9, ((1, 9, 11),)), (30, ((0, 30, 16),)), (11, ((0, 11, 13),)), (8, ()), (7, ((1, 7, 13), (2, 7, 31), (2, 4, 26), (2, 18, 22)))),
        (),
        ((10, ((0, 10, 12),)),),
        ((20, ()), (27, ((1, 27, 25), (0, 27, 15), (1, 5, 23))), (13, ())),
        ((15, ()), (14, ())),
        ((23, ()), (17, ((1, 17, 19),))),
        ((31, ((0, 31, 17), (0, 7, 19), (0, 23, 25))), (19, ())),
        ((28, ()), (26, ((1, 26, 24),)), (24, ()), (21, ((1, 21, 29),))),
        ((22, ()),),
        ((25, ()),),
        (),
        ((29, ()),),
        (),
    ),
)
ROWS = ((1, 1, 0, 0), (1, 0, 1, 0), (1, 1, 1, 1), (1, 1, 1, 1), (2, 1, 0, 1), (1, 1, 1, 1), (1, 2, 1, 0), (2, 1, 0, 1), (2, 2, 1, 0), (1, 1, 0, 0), (2, 1, 2, 1), (2, 2, 1, 1), (1, 0, 2, 0), (2, 2, 2, 2), (2, 2, 1, 1), (2, 2, 2, 2))

MASKED_TAIL = 15
MASKED_HEAD = 13

STEP_SLOTS = tuple((2 * e, 2 * e + 1) for e in range(16))


def kernel(
    q_hbm, k_hbm, v_hbm,
    out_hbm, key_low, key_step, value_low, value_step,
    kv, qv, qt, acc, top, stat, gathered, out_v,
    local_sems, recv_sems, send_sems, stat_send, stat_recv, out_sems,
):
    seq = lax.axis_index("seq")
    head = lax.axis_index("head")
    x = lax.rem(seq, XS)
    z = lax.div(seq, XS)
    xp = z * XS + lax.rem(x + 1, XS)
    xm = z * XS + lax.rem(x + XS - 1, XS)
    zp = lax.rem(z + 1, ZS) * XS + x
    zm = lax.rem(z + ZS - 1, ZS) * XS + x
    link = (xp, xm, zp)

    load_k = pltpu.make_async_copy(k_hbm, kv.at[pl.ds(OWN, 4), 0], local_sems.at[0])
    load_v = pltpu.make_async_copy(v_hbm, kv.at[pl.ds(OWN, 4), 1], local_sems.at[1])
    load_q = pltpu.make_async_copy(q_hbm, qv, local_sems.at[2])
    load_k.start()
    load_v.start()
    load_q.start()

    barrier = pltpu.get_barrier_semaphore()
    for other in (xp, xm, zp, zm):
        pl.semaphore_signal(
            barrier, inc=1, device_id={"seq": other, "head": head}, device_id_type=pl.DeviceIdType.MESH
        )
    peers = [lax.rem(head + d, KV_HEADS) for d in range(1, KV_HEADS)]
    for peer in peers:
        pl.semaphore_signal(
            barrier, inc=1, device_id={"seq": seq, "head": peer}, device_id_type=pl.DeviceIdType.MESH
        )
    load_k.wait()
    load_v.wait()
    pl.semaphore_wait(barrier, 4 + KV_HEADS - 1)

    def send(d, src, dst):
        pltpu.make_async_remote_copy(
            src_ref=kv.at[src],
            dst_ref=kv.at[dst],
            send_sem=send_sems.at[d],
            recv_sem=recv_sems.at[dst],
            device_id={"seq": link[d], "head": head},
            device_id_type=pl.DeviceIdType.MESH,
        ).start()

    def arrived(slot):
        pltpu.make_async_copy(kv.at[slot], kv.at[slot], recv_sems.at[slot]).wait()

    for here in range(XS):
        @pl.when(x == here)
        def _():
            for d, src, dst in STARTS[here]:
                send(d, src, dst)

    own_v = [kv[OWN + c, 1].T for c in range(4)]
    for c in range(4):
        part = own_v[c].astype(jnp.float32)
        stat[0:1, pl.ds(c * CHUNK, CHUNK)] = jnp.max(part, axis=0, keepdims=True)
        stat[1:2, pl.ds(c * CHUNK, CHUNK)] = jnp.min(part, axis=0, keepdims=True)
        keys = kv[OWN + c, 0].astype(jnp.float32)
        low = jnp.min(keys, axis=0, keepdims=True)
        key_low[pl.ds(c, 1), :] = low
        key_step[pl.ds(c, 1), :] = (jnp.max(keys, axis=0, keepdims=True) - low) / 3.0

    load_q.wait()
    for t in range(SPAN * PER):
        p, h = divmod(t, PER)
        part = qv[pl.ds(p * TILE, TILE), pl.ds(h * HEAD_DIM, HEAD_DIM)].T.astype(jnp.float32) * SCALE
        high = part.astype(jnp.bfloat16)
        qt[t, 0:HEAD_DIM, :] = high
        qt[t, HEAD_DIM:, :] = (part - high.astype(jnp.float32)).astype(jnp.bfloat16)

    ones = jnp.ones((16, 2 * CHUNK), jnp.bfloat16)

    def attend(slots, modes, first=False):
        keys = jnp.concatenate([kv[slots[0], 0], kv[slots[1], 0]], axis=0)
        keys = jnp.concatenate([keys, keys], axis=1)
        values = jnp.concatenate([kv[slots[0], 1].T, kv[slots[1], 1].T], axis=1)
        values = jnp.concatenate([values, ones], axis=0)
        for t in range(SPAN * PER):
            mode = modes[t // PER]
            if mode is None:
                continue
            s = jnp.dot(keys, qt[t], preferred_element_type=jnp.float32)
            if mode != "all":
                row = lax.broadcasted_iota(jnp.int32, s.shape, 0)
                col = lax.broadcasted_iota(jnp.int32, s.shape, 1)
                s = jnp.where(row <= col if mode == "past" else row > col, s, NEG)
            peak = jnp.max(s, axis=0, keepdims=True)
            if first:
                w = jnp.exp2(s - peak).astype(jnp.bfloat16)
                acc[t] = jnp.dot(values, w, preferred_element_type=jnp.float32)
                top[t] = peak
            else:
                old = top[t]
                new = jnp.maximum(old, peak)
                w = jnp.exp2(s - new).astype(jnp.bfloat16)
                part = jnp.dot(values, w, preferred_element_type=jnp.float32)
                acc[t] = acc[t] * jnp.exp2(old - new) + part
                top[t] = new

    attend((OWN, OWN + 1), ("past", "all"), first=True)

    for d, peer in enumerate(peers):
        pltpu.make_async_remote_copy(
            src_ref=stat,
            dst_ref=gathered.at[head],
            send_sem=stat_send.at[d],
            recv_sem=stat_recv.at[head],
            device_id={"seq": seq, "head": peer},
            device_id_type=pl.DeviceIdType.MESH,
        ).start()

    attend((OWN + 2, OWN + 3), (None, "past"))

    for e in range(16):
        for here in range(XS):
            @pl.when(x == here)
            def _():
                for slot, sends in STEPS[here][e]:
                    arrived(slot)
                    for d, src, dst in sends:
                        send(d, src, dst)
        rows = ROWS[e]
        modes = ("all", "all")
        if e == MASKED_HEAD:
            modes = ("all", "after")
        if e == MASKED_TAIL:
            modes = ("after", None)
        need = jnp.int32(rows[0])
        for here in range(1, XS):
            need = jnp.where(x == here, rows[here], need)

        @pl.when(z >= need)
        def _():
            attend(STEP_SLOTS[e], modes)

        if e == 5:
            most, least = stat[0:1, :], stat[1:2, :]
            for d in range(1, KV_HEADS):
                peer = peers[d - 1]
                pltpu.make_async_copy(gathered.at[peer], gathered.at[peer], stat_recv.at[peer]).wait()
                most = jnp.maximum(most, gathered[peer, 0:1, :])
                least = jnp.minimum(least, gathered[peer, 1:2, :])
            value_low[...] = least
            value_step[...] = (most - least) / 3.0

    copies = []
    for t in range(SPAN * PER):
        p, h = divmod(t, PER)
        full = acc[t]
        part = (full[0:HEAD_DIM] / full[HEAD_DIM : HEAD_DIM + 1]).astype(jnp.bfloat16)
        out_v[pl.ds(p * TILE, TILE), pl.ds(h * HEAD_DIM, HEAD_DIM)] = part.T
        if h == PER - 1:
            rows = pl.ds(p * TILE, TILE)
            copies.append(pltpu.make_async_copy(out_v.at[rows], out_hbm.at[rows], out_sems.at[p]))
            copies[-1].start()

    for d in range(KV_HEADS - 1):
        pltpu.make_async_copy(stat, stat, stat_send.at[d]).wait()
    for here in range(XS):
        @pl.when(x == here)
        def _():
            for d in range(3):
                count = sum(1 for s in STARTS[here] if s[0] == d)
                count += sum(1 for step in STEPS[here] for _, sends in step for s in sends if s[0] == d)
                block = kv.at[pl.ds(0, count)]
                pltpu.make_async_copy(block, block, send_sems.at[d]).wait()
    for copy in copies:
        copy.wait()


def shards(queries, new_keys, new_values):
    hbm = pl.BlockSpec(memory_space=pl.ANY)
    vmem = pl.BlockSpec(memory_space=pltpu.VMEM)
    f32, bf16 = jnp.float32, jnp.bfloat16
    tiles = SPAN * PER
    attended, key_low, key_step, value_low, value_step = pl.pallas_call(
        kernel,
        out_shape=(
            jax.ShapeDtypeStruct((TOK, PER * HEAD_DIM), bf16),
            jax.ShapeDtypeStruct((TOK // GROUP, HEAD_DIM), f32),
            jax.ShapeDtypeStruct((TOK // GROUP, HEAD_DIM), f32),
            jax.ShapeDtypeStruct((1, TOK), f32),
            jax.ShapeDtypeStruct((1, TOK), f32),
        ),
        in_specs=[hbm, hbm, hbm],
        out_specs=(hbm, vmem, vmem, vmem, vmem),
        scratch_shapes=[
            pltpu.VMEM((OWN + 4, 2, CHUNK, HEAD_DIM), bf16),
            pltpu.VMEM((TOK, PER * HEAD_DIM), bf16),
            pltpu.VMEM((tiles, 2 * HEAD_DIM, TILE), bf16),
            pltpu.VMEM((tiles, HEAD_DIM + 16, TILE), f32),
            pltpu.VMEM((tiles, 1, TILE), f32),
            pltpu.VMEM((2, TOK), f32),
            pltpu.VMEM((KV_HEADS, 2, TOK), f32),
            pltpu.VMEM((TOK, PER * HEAD_DIM), bf16),
            pltpu.SemaphoreType.DMA((3,)),
            pltpu.SemaphoreType.DMA((OWN,)),
            pltpu.SemaphoreType.DMA((3,)),
            pltpu.SemaphoreType.DMA((KV_HEADS - 1,)),
            pltpu.SemaphoreType.DMA((KV_HEADS,)),
            pltpu.SemaphoreType.DMA((SPAN,)),
        ],
        compiler_params=pltpu.CompilerParams(collective_id=0, has_side_effects=True),
    )(
        queries,
        new_keys.reshape(TOK // CHUNK, CHUNK, HEAD_DIM),
        new_values.reshape(TOK // CHUNK, CHUNK, HEAD_DIM),
    )
    return attended, key_low, key_step, value_low.reshape(TOK), value_step.reshape(TOK)


def solution(mesh):
    return jax.shard_map(
        shards,
        mesh=mesh,
        in_specs=(P("seq", "head"), P("seq", "head"), P("seq", "head")),
        out_specs=(P("seq", "head"), P("seq", "head"), P("seq", "head"), P("seq"), P("seq")),
        check_vma=False,
    )
```

time: 167 us -> 63 us (0.38)
  matrix products: 72.3 us -> 0 us
  Pallas kernels: 0 us -> 57.7 us
  waiting for transfers between devices: 47.6 us -> 0 us
  starting transfers between devices: 18.9 us -> 0 us
  other arithmetic: 18.7 us -> 0 us
  local copies, waits for them, and re-layouts: 6.94 us -> 4.43 us
    dot_general x18 -> x0, matrix products: 72.3 us -> none  [the longest x9 39.1 us: key_step(): jnp.einsum('hgqk,khd->hgqd', weights.astype(jnp.bfloat16), value_part, pr...]
    pallas_call x0 -> x1, Pallas kernels: none -> 57.7 us  [shards(): pl.pallas_call(kernel, out_shape=(jax.ShapeDtypeStruct((TOK, PER * HEAD_D...]
    ppermute x4 -> x0, waiting for transfers between devices: 38.3 us -> none  [passed_along(): return lax.ppermute(block, axis, route)]
    ppermute x4 -> x0, starting transfers between devices: 11.1 us -> none  [passed_along(): return lax.ppermute(block, axis, route)]
    reduce_sum x9 -> x0, other arithmetic: 9.53 us -> none  [key_step(): new_total = running_total * rescale + jnp.sum(weights, axis=-1)]
    all_to_all x2 -> x0, waiting for transfers between devices: 9.29 us -> none  [copy_for_each(): return lax.all_to_all(copies, axis, split_axis=0, concat_axis=0, tiled=True)]
    all_to_all x2 -> x0, starting transfers between devices: 7.81 us -> none  [copy_for_each(): return lax.all_to_all(copies, axis, split_axis=0, concat_axis=0, tiled=True)]
    concatenate x3 -> x0, other arithmetic: 3.07 us -> none  [shards(): context = jnp.concatenate((arrived, context), 1)]
  transfers between devices with their start and end apart: 6 -> 0, of which waited for: 5 -> 0; matrix products, arithmetic and copies ran while one was open for 3% -> 0% of each run, Pallas kernels for 0% -> 0%
where the time goes in v1:
time: 63 us; the launch traced here: 62.8 us
  Pallas kernels  57.7 us (92%)
  local copies, waits for them, and re-layouts  4.43 us (7%)
  between operations  0.65 us (1%)
    pallas_call x1, Pallas kernels, shards(): pl.pallas_call(kernel, out_shape=(jax.ShapeDtypeStruct((TOK, PER * HEAD_D...  57.7 us
    unnamed x13, local copies, waits for them, and re-layouts  4.43 us

profile of v1, /device:TPU:160, one launch (start us, length us, event | category | flops | bytes accessed | tf_op | source)
XLA Modules:
  0.0 62.8 jit_solution(3295890290276809734)
XLA Ops:
  0.6 57.7 %shard_map.74 = (bf16[512,512]{1,0:T(8,128)(2,1)}, f32[4,128]{1,0:T(4,128)}, f32[4,128]{1,0:T(4,128)}, f32[1,512]{1,0:T(1,128)}, f32[1,512]{1,0:T(1,128)}) custom-call(bf16[512,512]{1,0:T(8,128)(2,1)} %q_hbm.1, bf16[4,128,128]{2,1,0:T(8,128)(2,1)} %bitcast.4, bf16[4,128,128]{2,1,0:T(8,128)(2,1)} %bitcast.5), custom_call_target="tpu_custom_call" | custom-call | tf_op jit(solution)/shard_map/pallas_call | solution.py:295
  58.4 0.0 copy-start.3
  58.4 1.9 %copy.13 = bf16[512,512]{1,0:T(8,128)(2,1)} copy(bf16[512,512]{1,0:T(8,128)(2,1)} %get-tuple-element.20) | data formatting | bytes 1048576
  60.2 0.0 copy-done.3
  60.2 0.0 copy-start.2
  60.3 0.6 copy.14
  60.8 0.1 copy-done.2
  60.9 0.0 copy-start.1
  60.9 0.6 copy.15
  61.5 0.1 copy-done.1
  61.6 0.0 copy-start
  61.6 0.6 copy.16
  62.2 0.1 copy-done
  62.2 0.6 copy.17
Async XLA Ops:
  58.4 1.9 %copy-start.3 = (f32[4,128]{1,0:T(4,128)S(1)}, f32[4,128]{1,0:T(4,128)}, u32[]{:S(2)}) copy-start(f32[4,128]{1,0:T(4,128)} %get-tuple-element.21) | copy-start | bytes 6148
  60.2 0.7 %copy-start.2 = (f32[4,128]{1,0:T(4,128)S(1)}, f32[4,128]{1,0:T(4,128)}, u32[]{:S(2)}) copy-start(f32[4,128]{1,0:T(4,128)} %get-tuple-element.22) | copy-start | bytes 6148
  60.9 0.7 %copy-start.1 = (f32[1,512]{1,0:T(1,128)S(1)}, f32[1,512]{1,0:T(1,128)}, u32[]{:S(2)}) copy-start(f32[1,512]{1,0:T(1,128)} %get-tuple-element.13) | copy-start | bytes 6148
  61.6 0.6 %copy-start = (f32[1,512]{1,0:T(1,128)S(1)}, f32[1,512]{1,0:T(1,128)}, u32[]{:S(2)}) copy-start(f32[1,512]{1,0:T(1,128)} %get-tuple-element.14) | copy-start | bytes 6148

commit v2 on v0

v2 whole, which is shorter than its diff:
```python
import math

import jax
import jax.numpy as jnp
from jax import lax
from jax.experimental import pallas as pl
from jax.experimental.pallas import tpu as pltpu
from jax.sharding import PartitionSpec as P

HEADS = 32
KV_HEADS = 8
HEAD_DIM = 128
WINDOW = 4096
GROUP = 128
PER = HEADS // KV_HEADS
TOK = 512
CHUNK = 128
TILE = 256
TILES = TOK // TILE * PER
DEEP = HEAD_DIM + 16
XS = 4
ZS = 8
OWN = 32
STEPS = 16
SCALE = 1.4426950408889634 / math.sqrt(HEAD_DIM)
NEG = -1e30
MESH = pl.DeviceIdType.MESH

PLAN = (
    (
        (2056, 6146, 10240, 2241, 6211, 10305, 2176, 6296, 10372, 12288, 4, 4104, 8222, 10437, 12352, 69, 4169, 8287, 12544, 270, 4372, 2121, 8476, 12480, 13504, 5327, 14208, 12416, 12672, 4496, 12608, 335, 8541, 12800, 12736, 4561, 8651, 4437, 6361, 14272, 12864, 595, 13056, 8982, 8785, 14080, 13184, 916, 13824, 14144, 13312, 1050, 12928, 12992, 13120, 9047, 14016, 13696, 13248, 13568, 13376, 13440, 13632, 13760, 13888, 13952),
        (9, 18, 28, 33, 39, 42, 54, 56, 59, 61, 62, 63, 64, 65, 66, 66, 66),
        (1, 1, 1, 1, 1, 2, 1, 2, 2, 1, 2, 2, 1, 2, 2, 2),
        (11, 11, 12),
    ),
    (
        (2121, 10443, 2241, 10242, 2176, 10307, 12800, 526, 12992, 4819, 8925, 12352, 12416, 4230, 140, 8350, 12288, 16, 2056, 12480, 4295, 8415, 10378, 205, 13824, 5644, 12544, 14144, 12672, 4504, 8592, 12608, 14208, 6026, 5979, 12736, 8657, 13184, 918, 81, 14272, 13120, 12864, 12928, 8860, 9750, 13056, 13248, 983, 13312, 5140, 13440, 13376, 5205, 13504, 1243, 9435, 13632, 14080, 5914, 13568, 13760, 13696, 13952, 13888, 14016),
        (6, 19, 24, 32, 37, 43, 46, 47, 49, 54, 57, 61, 63, 65, 66, 66, 66),
        (0, 1, 1, 1, 0, 1, 1, 1, 2, 1, 2, 2, 1, 2, 2, 2),
        (12, 10, 12),
    ),
    (
        (2048, 10372, 2113, 10242, 2253, 10307, 10437, 12864, 603, 12544, 4376, 12352, 12416, 4230, 138, 8350, 83, 12288, 8212, 12480, 4295, 12736, 4557, 8659, 13184, 12608, 343, 2188, 8541, 8476, 8415, 8277, 12672, 4492, 13056, 14208, 13952, 5778, 13312, 13568, 1294, 18, 12928, 12800, 538, 13504, 5333, 12992, 13120, 14144, 5975, 4441, 13824, 13696, 14080, 13248, 13376, 14272, 13440, 13760, 13632, 13888, 14016),
        (7, 19, 21, 32, 34, 45, 48, 49, 56, 57, 59, 61, 61, 62, 63, 63, 63),
        (0, 1, 1, 1, 0, 1, 1, 0, 0, 2, 1, 1, 2, 1, 2, 2),
        (11, 9, 11),
    ),
    (
        (10309, 10244, 10374, 10439, 12288, 12416, 12608, 323, 4423, 12352, 12480, 12544, 258, 4358, 8478, 13120, 13824, 12672, 392, 4506, 8604, 8267, 8543, 14016, 12800, 4618, 12736, 457, 8669, 12928, 12864, 4683, 14208, 1934, 13504, 13568, 14080, 1808, 5912, 4303, 6034, 13760, 1485, 13248, 12992, 13056, 8982, 13312, 14272, 1999, 13184, 914, 729, 13376, 14144, 5977, 13440, 13632, 13696, 13952, 13888),
        (4, 10, 11, 15, 29, 32, 45, 47, 53, 54, 57, 58, 59, 61, 61, 61, 61),
        (0, 0, 1, 1, 1, 1, 0, 1, 1, 0, 1, 1, 0, 0, 2, 2),
        (10, 9, 10),
    ),
)
OPS = max(len(plan[0]) for plan in PLAN)


def kernel(
    q_hbm, k_hbm, v_hbm,
    acc, key_stats, value_stats,
    kv, qv, qt, scores, weights, factor, top, held, stat, gathered, ops, bounds, rows,
    local_sems, recv_sems, send_sems, stat_send, stat_recv,
):
    seq = lax.axis_index("seq")
    head = lax.axis_index("head")
    x = lax.rem(seq, XS)
    z = lax.div(seq, XS)
    xp = z * XS + lax.rem(x + 1, XS)
    xm = z * XS + lax.rem(x + XS - 1, XS)
    zp = lax.rem(z + 1, ZS) * XS + x
    zm = lax.rem(z + ZS - 1, ZS) * XS + x
    peers = [lax.rem(head + d, KV_HEADS) for d in range(1, KV_HEADS)]

    load_k = pltpu.make_async_copy(k_hbm, kv.at[pl.ds(OWN, 4), 0], local_sems.at[0])
    load_v = pltpu.make_async_copy(v_hbm, kv.at[pl.ds(OWN, 4), 1], local_sems.at[1])
    load_q = pltpu.make_async_copy(q_hbm, qv, local_sems.at[2])
    load_k.start()
    load_v.start()
    load_q.start()

    barrier = pltpu.get_barrier_semaphore()
    for other in (xp, xm, zp, zm):
        pl.semaphore_signal(barrier, inc=1, device_id={"seq": other, "head": head}, device_id_type=MESH)
    for peer in peers:
        pl.semaphore_signal(barrier, inc=1, device_id={"seq": seq, "head": peer}, device_id_type=MESH)

    for here in range(XS):
        @pl.when(x == here)
        def _():
            plan_ops, plan_bounds, plan_rows, _ = PLAN[here]
            for i, value in enumerate(plan_ops):
                ops[i] = value
            for i, value in enumerate(plan_bounds):
                bounds[i] = value
            for i, value in enumerate(plan_rows):
                rows[i] = value

    load_k.wait()
    load_v.wait()
    pl.semaphore_wait(barrier, 4 + KV_HEADS - 1)

    def operate(i, carry):
        value = ops[i]
        kind = lax.div(value, 4096)
        src = lax.rem(lax.div(value, 64), 64)
        dst = lax.rem(value, 64)

        @pl.when(kind == 3)
        def _():
            pltpu.make_async_copy(kv.at[src], kv.at[src], recv_sems.at[src]).wait()

        @pl.when(kind < 3)
        def _():
            there = jnp.where(kind == 0, xp, jnp.where(kind == 1, xm, zp))
            pltpu.make_async_remote_copy(
                src_ref=kv.at[src],
                dst_ref=kv.at[dst],
                send_sem=send_sems.at[kind],
                recv_sem=recv_sems.at[dst],
                device_id={"seq": there, "head": head},
                device_id_type=MESH,
            ).start()

        return carry

    lax.fori_loop(0, bounds[0], operate, 0)

    for c in range(4):
        part = kv[OWN + c, 1].T.astype(jnp.float32)
        stat[0:1, pl.ds(c * CHUNK, CHUNK)] = jnp.max(part, axis=0, keepdims=True)
        stat[1:2, pl.ds(c * CHUNK, CHUNK)] = jnp.min(part, axis=0, keepdims=True)
        keys = kv[OWN + c, 0].astype(jnp.float32)
        low = jnp.min(keys, axis=0, keepdims=True)
        key_stats[pl.ds(c, 1), :] = low
        key_stats[pl.ds(4 + c, 1), :] = (jnp.max(keys, axis=0, keepdims=True) - low) / 3.0

    load_q.wait()
    for t in range(TILES):
        p, h = divmod(t, PER)
        part = qv[pl.ds(p * TILE, TILE), pl.ds(h * HEAD_DIM, HEAD_DIM)].T.astype(jnp.float32) * SCALE
        high = part.astype(jnp.bfloat16)
        qt[t, 0:HEAD_DIM, :] = high
        qt[t, HEAD_DIM:, :] = (part - high.astype(jnp.float32)).astype(jnp.bfloat16)
        top[t] = jnp.full((1, TILE), NEG, jnp.float32)
        acc[t] = jnp.zeros((DEEP, TILE), jnp.float32)

    def score(keys, t, mode):
        s = jnp.dot(keys, qt[t], preferred_element_type=jnp.float32)
        if mode != "all":
            row = lax.broadcasted_iota(jnp.int32, s.shape, 0)
            col = lax.broadcasted_iota(jnp.int32, s.shape, 1)
            s = jnp.where(row <= col if mode == "past" else row > col, s, NEG)
        scores[t] = s

    def weigh(t):
        s = scores[t]
        old = top[t]
        new = jnp.maximum(old, jnp.max(s, axis=0, keepdims=True))
        weights[t] = jnp.exp2(s - new).astype(jnp.bfloat16)
        factor[t] = jnp.exp2(old - new)
        top[t] = new

    def gather(values, t):
        acc[t] = acc[t] * factor[t] + jnp.dot(values, weights[t], preferred_element_type=jnp.float32)

    def attend(first, second, modes, before=True, after=True):
        past = held[...]
        keys = jnp.concatenate([kv[first, 0], kv[second, 0]], axis=0)
        keys = jnp.concatenate([keys, keys], axis=1)
        values = jnp.concatenate([kv[first, 1].T, kv[second, 1].T], axis=1)
        values = jnp.concatenate([values, jnp.ones((DEEP - HEAD_DIM, 2 * CHUNK), jnp.bfloat16)], axis=0)
        jobs = [t for t in range(TILES) if modes[t // PER] is not None]
        to_weigh = ([6, 7] if before else [None, None]) + jobs
        to_gather = ([4, 5, 6, 7] if before else [None] * 4) + jobs
        for i, t in enumerate(jobs):
            score(keys, t, modes[t // PER])
            if to_weigh[i] is not None:
                weigh(to_weigh[i])
            if to_gather[i] is not None:
                gather(past if i < 4 else values, to_gather[i])
        if after:
            held[...] = values
        else:
            for t in to_weigh[len(jobs):]:
                weigh(t)
            for t in to_gather[len(jobs):]:
                gather(values, t)

    attend(OWN, OWN + 1, ("past", "all"), before=False)

    for d, peer in enumerate(peers):
        pltpu.make_async_remote_copy(
            src_ref=stat,
            dst_ref=gathered.at[head],
            send_sem=stat_send.at[d],
            recv_sem=stat_recv.at[head],
            device_id={"seq": seq, "head": peer},
            device_id_type=MESH,
        ).start()

    attend(OWN + 2, OWN + 3, (None, "past"))

    def step(e, carry):
        lax.fori_loop(bounds[e], bounds[e + 1], operate, 0)

        @pl.when(z >= rows[e])
        def _():
            attend(2 * e, 2 * e + 1, ("all", "all"))

        return carry

    lax.fori_loop(0, STEPS - 2, step, 0)

    most, least = stat[0:1, :], stat[1:2, :]
    for peer in peers:
        pltpu.make_async_copy(gathered.at[peer], gathered.at[peer], stat_recv.at[peer]).wait()
        most = jnp.maximum(most, gathered[peer, 0:1, :])
        least = jnp.minimum(least, gathered[peer, 1:2, :])
    value_stats[0:1, :] = least
    value_stats[1:2, :] = (most - least) / 3.0

    lax.fori_loop(bounds[STEPS - 2], bounds[STEPS], operate, 0)

    @pl.when(z >= 2)
    def _():
        attend(2 * STEPS - 4, 2 * STEPS - 3, ("all", "after"))
        attend(2 * STEPS - 2, 2 * STEPS - 1, ("after", None), after=False)

    @pl.when(z < 2)
    def _():
        past = held[...]
        for t in (6, 7):
            weigh(t)
        for t in (4, 5, 6, 7):
            gather(past, t)

    for d in range(KV_HEADS - 1):
        pltpu.make_async_copy(stat, stat, stat_send.at[d]).wait()
    for here in range(XS):
        @pl.when(x == here)
        def _():
            for d, count in enumerate(PLAN[here][3]):
                block = kv.at[pl.ds(0, count)]
                pltpu.make_async_copy(block, block, send_sems.at[d]).wait()


def finish(acc, key_stats, value_stats, out_hbm, key_low, key_step, value_low, value_step, out_v, sems):
    copies = []
    for t in range(TILES):
        p, h = divmod(t, PER)
        part = acc[t, 0:HEAD_DIM] / acc[t, HEAD_DIM : HEAD_DIM + 1]
        out_v[pl.ds(p * TILE, TILE), pl.ds(h * HEAD_DIM, HEAD_DIM)] = part.astype(jnp.bfloat16).T
        if h == PER - 1:
            block = pl.ds(p * TILE, TILE)
            copies.append(pltpu.make_async_copy(out_v.at[block], out_hbm.at[block], sems.at[p]))
            copies[-1].start()
    key_low[...] = key_stats[0:4, :]
    key_step[...] = key_stats[4:8, :]
    value_low[...] = value_stats[0:1, :]
    value_step[...] = value_stats[1:2, :]
    for copy in copies:
        copy.wait()


def shards(queries, new_keys, new_values):
    hbm = pl.BlockSpec(memory_space=pl.ANY)
    vmem = pl.BlockSpec(memory_space=pltpu.VMEM)
    f32, bf16 = jnp.float32, jnp.bfloat16
    chunks = TOK // CHUNK
    state = pl.pallas_call(
        kernel,
        out_shape=(
            pltpu.VMEM((TILES, DEEP, TILE), f32),
            pltpu.VMEM((2 * chunks, HEAD_DIM), f32),
            pltpu.VMEM((2, TOK), f32),
        ),
        in_specs=[hbm, hbm, hbm],
        out_specs=(vmem, vmem, vmem),
        scratch_shapes=[
            pltpu.VMEM((OWN + 4, 2, CHUNK, HEAD_DIM), bf16),
            pltpu.VMEM((TOK, PER * HEAD_DIM), bf16),
            pltpu.VMEM((TILES, 2 * HEAD_DIM, TILE), bf16),
            pltpu.VMEM((TILES, 2 * CHUNK, TILE), f32),
            pltpu.VMEM((TILES, 2 * CHUNK, TILE), bf16),
            pltpu.VMEM((TILES, 1, TILE), f32),
            pltpu.VMEM((TILES, 1, TILE), f32),
            pltpu.VMEM((DEEP, 2 * CHUNK), bf16),
            pltpu.VMEM((2, TOK), f32),
            pltpu.VMEM((KV_HEADS, 2, TOK), f32),
            pltpu.SMEM((OPS,), jnp.int32),
            pltpu.SMEM((STEPS + 1,), jnp.int32),
            pltpu.SMEM((STEPS,), jnp.int32),
            pltpu.SemaphoreType.DMA((3,)),
            pltpu.SemaphoreType.DMA((OWN,)),
            pltpu.SemaphoreType.DMA((3,)),
            pltpu.SemaphoreType.DMA((KV_HEADS - 1,)),
            pltpu.SemaphoreType.DMA((KV_HEADS,)),
        ],
        compiler_params=pltpu.CompilerParams(collective_id=0, has_side_effects=True),
    )(
        queries,
        new_keys.reshape(chunks, CHUNK, HEAD_DIM),
        new_values.reshape(chunks, CHUNK, HEAD_DIM),
    )
    state = [pltpu.with_memory_space_constraint(part, pltpu.VMEM) for part in state]
    attended, key_low, key_step, value_low, value_step = pl.pallas_call(
        finish,
        out_shape=(
            jax.ShapeDtypeStruct((TOK, PER * HEAD_DIM), bf16),
            jax.ShapeDtypeStruct((TOK // GROUP, HEAD_DIM), f32),
            jax.ShapeDtypeStruct((TOK // GROUP, HEAD_DIM), f32),
            jax.ShapeDtypeStruct((1, TOK), f32),
            jax.ShapeDtypeStruct((1, TOK), f32),
        ),
        in_specs=[vmem, vmem, vmem],
        out_specs=(hbm, vmem, vmem, vmem, vmem),
        scratch_shapes=[
            pltpu.VMEM((TOK, PER * HEAD_DIM), bf16),
            pltpu.SemaphoreType.DMA((TOK // TILE,)),
        ],
    )(*state)
    return attended, key_low, key_step, value_low.reshape(TOK), value_step.reshape(TOK)


def solution(mesh):
    return jax.shard_map(
        shards,
        mesh=mesh,
        in_specs=(P("seq", "head"), P("seq", "head"), P("seq", "head")),
        out_specs=(P("seq", "head"), P("seq", "head"), P("seq", "head"), P("seq"), P("seq")),
        check_vma=False,
    )
```

time: 167 us -> 33.7 us (0.20)
  matrix products: 72.3 us -> 0 us
  waiting for transfers between devices: 47.6 us -> 0 us
  Pallas kernels: 0 us -> 32.4 us
  starting transfers between devices: 18.9 us -> 0 us
  other arithmetic: 18.7 us -> 0 us
  local copies, waits for them, and re-layouts: 6.94 us -> 0 us
    dot_general x18 -> x0, matrix products: 72.3 us -> none  [the longest x9 39.1 us: key_step(): jnp.einsum('hgqk,khd->hgqd', weights.astype(jnp.bfloat16), value_part, pr...]
    ppermute x4 -> x0, waiting for transfers between devices: 38.3 us -> none  [passed_along(): return lax.ppermute(block, axis, route)]
    pallas_call x0 -> x2, Pallas kernels: none -> 32.4 us  [the longest x1 30.9 us: shards(): pl.pallas_call(kernel, out_shape=(pltpu.VMEM((TILES, DEEP, TILE), f32), p...]
    ppermute x4 -> x0, starting transfers between devices: 11.1 us -> none  [passed_along(): return lax.ppermute(block, axis, route)]
    reduce_sum x9 -> x0, other arithmetic: 9.53 us -> none  [key_step(): new_total = running_total * rescale + jnp.sum(weights, axis=-1)]
    all_to_all x2 -> x0, waiting for transfers between devices: 9.29 us -> none  [copy_for_each(): return lax.all_to_all(copies, axis, split_axis=0, concat_axis=0, tiled=True)]
    all_to_all x2 -> x0, starting transfers between devices: 7.81 us -> none  [copy_for_each(): return lax.all_to_all(copies, axis, split_axis=0, concat_axis=0, tiled=True)]
    unnamed x19 -> x0, local copies, waits for them, and re-layouts: 5.24 us -> none
  transfers between devices with their start and end apart: 6 -> 0, of which waited for: 5 -> 0; matrix products, arithmetic and copies ran while one was open for 3% -> 0% of each run, Pallas kernels for 0% -> 0%
where the time goes in v2:
time: 33.7 us; the launch traced here: 33 us
  Pallas kernels  32.4 us (96%)
  between operations  0.64 us (2%)
    pallas_call x1, Pallas kernels, shards(): pl.pallas_call(kernel, out_shape=(pltpu.VMEM((TILES, DEEP, TILE), f32), p...  30.9 us
    pallas_call x1, Pallas kernels, shards(): pl.pallas_call(finish, out_shape=(jax.ShapeDtypeStruct((TOK, PER * HEAD_D...  1.53 us

profile of v2, /device:TPU:160, one launch (start us, length us, event | category | flops | bytes accessed | tf_op | source)
XLA Modules:
  0.0 33.0 jit_solution(3785725109228447459)
XLA Ops:
  0.6 30.9 %shard_map.74 = (f32[8,144,256]{2,1,0:T(8,128)S(1)}, f32[8,128]{1,0:T(8,128)S(1)}, f32[2,512]{1,0:T(2,128)S(1)}) custom-call(bf16[512,512]{1,0:T(8,128)(2,1)} %q_hbm.1, bf16[4,128,128]{2,1,0:T(8,128)(2,1)} %bitcast.4, bf16[4,128,128]{2,1,0:T(8,128)(2,1)} %bitcast.5), custom_call_target="tpu_custom_call" | custom-call | tf_op jit(solution)/shard_map/pallas_call | solution.py:270
  31.5 1.5 %shard_map.75 = (bf16[512,512]{1,0:T(8,128)(2,1)}, f32[4,128]{1,0:T(4,128)}, f32[4,128]{1,0:T(4,128)}, f32[1,512]{1,0:T(1,128)}, f32[1,512]{1,0:T(1,128)}) custom-call(f32[8,144,256]{2,1,0:T(8,128)S(1)} %get-tuple-element.13.acc, f32[8,128]{1,0:T(8,128)S(1)} %get-tuple-element.14.key_stats, f32[2,512]{1,0:T(2,128)S(1)} %get-tuple-element.15.value_stats), custom_call_target="tpu_custom_call" | custom-call | tf_op jit(solution)/shard_map/pallas_call | solution.py:306

commit v3 on v2

v3 whole, which is shorter than its diff:
```python
import math

import jax
import jax.numpy as jnp
from jax import lax
from jax.experimental import pallas as pl
from jax.experimental.pallas import tpu as pltpu
from jax.sharding import PartitionSpec as P

HEADS = 32
KV_HEADS = 8
HEAD_DIM = 128
WINDOW = 4096
GROUP = 128
PER = HEADS // KV_HEADS
TOK = 512
CHUNK = 128
TILE = 256
TILES = TOK // TILE * PER
DEEP = HEAD_DIM + 16
XS = 4
ZS = 8
REACH = 3
OWN = 32
STEPS = 15
SCALE = 1.4426950408889634 / math.sqrt(HEAD_DIM)
NEG = -1e30
MESH = pl.DeviceIdType.MESH

PLAN = (
    (
        (34881, 18434, 2255, 34816, 2121, 18631, 18499, 35011, 53312, 34946, 18566, 4163, 20557, 36941, 53248, 4098, 20492, 36876, 53440, 4299, 20689, 37071, 53632, 53568, 4437, 53376, 4234, 20624, 37006, 54272, 53504, 2190, 4372, 58176, 53696, 20957, 37331, 53824, 58112, 58496, 53760, 4632, 37404, 58304, 53952, 21211, 37595, 53888, 37530, 58240, 54336, 58816, 58560, 54528, 38174, 54592, 59136, 10014, 58880, 58752, 59072, 58944, 59008, 59200, 59328, 59264),
        (8, 18, 29, 33, 37, 43, 49, 50, 53, 55, 58, 60, 62, 63, 64, 66),
        (1, 1, 1, 1, 1, 1, 2, 1, 2, 1, 2, 2, 2, 2, 2),
        ((3, 7, 1), (4, 6, 0), (4, 9, 0)),
        6,
    ),
    (
        (2241, 2176, 34944, 34820, 2117, 2052, 35009, 50112, 991, 53248, 4104, 20486, 36882, 49728, 34885, 53504, 4368, 20752, 37136, 53312, 20551, 36947, 53440, 53696, 58496, 25746, 53376, 4238, 54080, 21323, 37723, 53568, 4433, 20817, 37201, 53952, 53632, 20884, 37270, 58368, 25624, 54592, 5461, 38237, 49664, 58560, 53888, 54016, 59072, 9945, 50048, 926, 54848, 38495, 58432, 25689, 54528, 58816, 26079, 58752, 54784, 59008, 59200, 59136, 59328, 59264),
        (7, 22, 28, 35, 39, 45, 47, 48, 52, 56, 57, 60, 61, 63, 64, 66),
        (1, 1, 1, 1, 0, 1, 1, 0, 2, 1, 2, 1, 2, 2, 2),
        ((6, 5, 1), (0, 6, 4), (4, 8, 0)),
        8,
    ),
    (
        (35011, 34887, 34946, 2068, 2249, 49216, 34822, 75, 32841, 53440, 2184, 20679, 37083, 49152, 10, 53696, 20941, 49472, 339, 53376, 4238, 20614, 37018, 49792, 17032, 49408, 274, 53632, 20876, 37272, 54528, 2133, 38162, 51136, 34775, 53824, 54080, 21337, 37725, 53760, 59072, 26327, 49856, 54272, 5150, 59008, 54016, 37660, 54144, 58880, 26138, 54208, 58496, 25756, 54336, 58560, 54720, 54592, 54656, 59200, 58944, 59136, 51072),
        (5, 15, 23, 27, 30, 40, 43, 48, 52, 55, 56, 58, 59, 61, 63, 63),
        (0, 1, 0, 1, 1, 0, 1, 1, 1, 2, 1, 1, 2, 2, 0),
        ((8, 2, 0), (1, 5, 3), (6, 6, 0)),
        12,
    ),
    (
        (34881, 34816, 35013, 50432, 34948, 34074, 53312, 4165, 36951, 49280, 16522, 49728, 33359, 53248, 4100, 20500, 36886, 49600, 53568, 4425, 20813, 37209, 49344, 16587, 49856, 53504, 4360, 20748, 37144, 49536, 49664, 54912, 5770, 54080, 21327, 49792, 33436, 58816, 9687, 26067, 54016, 50368, 34015, 54208, 5077, 54336, 54144, 58752, 9622, 54272, 21526, 50304, 58944, 9821, 55104, 50496, 58880, 54976, 55168, 55040, 55232),
        (3, 17, 24, 29, 31, 33, 37, 41, 47, 51, 52, 56, 57, 59, 60, 61),
        (1, 0, 1, 0, 0, 0, 1, 1, 1, 0, 0, 2, 1, 1, 1),
        ((0, 6, 3), (2, 5, 1), (8, 4, 0)),
        11,
    ),
)
OPS = max(len(plan[0]) for plan in PLAN)
TAIL_OUT = ((2, 3), (0, 1, 2, 3))
FULL_OUT = ((6, 7), (4, 5, 6, 7))


def kernel(
    q_hbm, k_hbm, v_hbm,
    acc, key_low, key_step, value_low, value_step,
    kv, qv, qt, scores, weights, factor, top, held, stat, gathered, ops, bounds, rows,
    local_sems, recv_sems, send_sems, stat_send, stat_recv,
):
    seq = lax.axis_index("seq")
    head = lax.axis_index("head")
    x = lax.rem(seq, XS)
    z = lax.div(seq, XS)
    xp = z * XS + lax.rem(x + 1, XS)
    xm = z * XS + lax.rem(x + XS - 1, XS)
    first_row, last_row = z == 0, z == ZS - 1
    zp = jnp.where(last_row, seq, seq + XS)
    zm = jnp.where(first_row, seq, seq - XS)
    peers = [lax.rem(head + d, KV_HEADS) for d in range(1, KV_HEADS)]

    load_k = pltpu.make_async_copy(k_hbm, kv.at[pl.ds(OWN, 4), 0], local_sems.at[0])
    load_v = pltpu.make_async_copy(v_hbm, kv.at[pl.ds(OWN, 4), 1], local_sems.at[1])
    load_q = pltpu.make_async_copy(q_hbm, qv, local_sems.at[2])
    load_k.start()
    load_v.start()
    load_q.start()

    barrier = pltpu.get_barrier_semaphore()

    def greet(other):
        pl.semaphore_signal(barrier, inc=1, device_id={"seq": other, "head": head}, device_id_type=MESH)

    greet(xp)
    greet(xm)

    @pl.when(jnp.logical_not(last_row))
    def _():
        greet(zp)

    @pl.when(jnp.logical_not(first_row))
    def _():
        greet(zm)

    for peer in peers:
        pl.semaphore_signal(barrier, inc=1, device_id={"seq": seq, "head": peer}, device_id_type=MESH)

    for here in range(XS):
        @pl.when(x == here)
        def _():
            for table, values in zip((ops, bounds, rows), PLAN[here]):
                for i, value in enumerate(values):
                    table[i] = value

    load_k.wait()
    load_v.wait()
    ends = jnp.where(jnp.logical_or(first_row, last_row), 1, 0)
    pl.semaphore_wait(barrier, 4 + KV_HEADS - 1 - ends)

    def operate(i, carry):
        value = ops[i]
        kind = lax.div(value, 16384)
        row = lax.rem(lax.div(value, 4096), 4)
        src = lax.rem(lax.div(value, 64), 64)
        dst = lax.rem(value, 64)
        here = z >= row

        @pl.when(jnp.logical_and(kind == 3, here))
        def _():
            pltpu.make_async_copy(kv.at[src], kv.at[src], recv_sems.at[src]).wait()

        wanted = jnp.logical_or(kind < 2, jnp.logical_and(kind == 2, z < ZS - 1))

        @pl.when(jnp.logical_and(wanted, here))
        def _():
            there = jnp.where(kind == 0, xp, jnp.where(kind == 1, xm, zp))
            pltpu.make_async_remote_copy(
                src_ref=kv.at[src],
                dst_ref=kv.at[dst],
                send_sem=send_sems.at[kind, row],
                recv_sem=recv_sems.at[dst],
                device_id={"seq": there, "head": head},
                device_id_type=MESH,
            ).start()

        return carry

    lax.fori_loop(0, bounds[0], operate, 0)
    pair = jnp.int32(PLAN[0][4])
    for here in range(1, XS):
        pair = jnp.where(x == here, PLAN[here][4], pair)

    for c in range(4):
        part = kv[OWN + c, 1].T.astype(jnp.float32)
        stat[0:1, pl.ds(c * CHUNK, CHUNK)] = jnp.max(part, axis=0, keepdims=True)
        stat[1:2, pl.ds(c * CHUNK, CHUNK)] = jnp.min(part, axis=0, keepdims=True)
        keys = kv[OWN + c, 0].astype(jnp.float32)
        low = jnp.min(keys, axis=0, keepdims=True)
        key_low[pl.ds(c, 1), :] = low
        key_step[pl.ds(c, 1), :] = (jnp.max(keys, axis=0, keepdims=True) - low) / 3.0

    load_q.wait()
    for t in range(TILES):
        p, h = divmod(t, PER)
        part = qv[pl.ds(p * TILE, TILE), pl.ds(h * HEAD_DIM, HEAD_DIM)].T.astype(jnp.float32) * SCALE
        high = part.astype(jnp.bfloat16)
        qt[t, 0:HEAD_DIM, :] = high
        qt[t, HEAD_DIM:, :] = (part - high.astype(jnp.float32)).astype(jnp.bfloat16)
        top[t] = jnp.full((1, TILE), NEG, jnp.float32)
        acc[t] = jnp.zeros((DEEP, TILE), jnp.float32)

    def score(keys, t, mode):
        s = jnp.dot(keys, qt[t], preferred_element_type=jnp.float32)
        if mode != "all":
            row = lax.broadcasted_iota(jnp.int32, s.shape, 0)
            col = lax.broadcasted_iota(jnp.int32, s.shape, 1)
            s = jnp.where(row <= col if mode == "past" else row > col, s, NEG)
        scores[t] = s

    def weigh(t):
        s = scores[t]
        old = top[t]
        new = jnp.maximum(old, jnp.max(s, axis=0, keepdims=True))
        weights[t] = jnp.exp2(s - new).astype(jnp.bfloat16)
        factor[t] = jnp.exp2(old - new)
        top[t] = new

    def gather(values, t):
        acc[t] = acc[t] * factor[t] + jnp.dot(values, weights[t], preferred_element_type=jnp.float32)

    def attend(first, second, modes, before=FULL_OUT):
        past = held[...]
        keys = jnp.concatenate([kv[first, 0], kv[second, 0]], axis=0)
        keys = jnp.concatenate([keys, keys], axis=1)
        values = jnp.concatenate([kv[first, 1].T, kv[second, 1].T], axis=1)
        values = jnp.concatenate([values, jnp.ones((DEEP - HEAD_DIM, 2 * CHUNK), jnp.bfloat16)], axis=0)
        jobs = tuple(t for t in range(TILES) if modes[t // PER] is not None)
        to_weigh = before[0] + jobs
        to_gather = before[1] + jobs
        for i, t in enumerate(jobs):
            score(keys, t, modes[t // PER])
            if to_weigh[i] is not None:
                weigh(to_weigh[i])
            if to_gather[i] is not None:
                gather(past if i < 4 else values, to_gather[i])
        held[...] = values

    attend(OWN, OWN + 1, ("past", "all"), before=((None,) * 2, (None,) * 4))

    for d, peer in enumerate(peers):
        pltpu.make_async_remote_copy(
            src_ref=stat,
            dst_ref=gathered.at[head],
            send_sem=stat_send.at[d],
            recv_sem=stat_recv.at[head],
            device_id={"seq": seq, "head": peer},
            device_id_type=MESH,
        ).start()

    attend(OWN + 2, OWN + 3, (None, "past"))

    def step(e, carry):
        lax.fori_loop(bounds[e], bounds[e + 1], operate, 0)
        slot = 2 * e + jnp.where(e > pair, 2, 0)
        there = z >= rows[e]

        @pl.when(jnp.logical_and(there, e != pair))
        def _():
            attend(slot, slot + 1, ("all", "all"))

        @pl.when(jnp.logical_and(there, e == pair))
        def _():
            attend(slot, slot + 1, ("after", None))
            attend(slot + 2, slot + 3, ("all", "after"), before=TAIL_OUT)

        return carry

    lax.fori_loop(0, STEPS - 1, step, 0)

    most, least = stat[0:1, :], stat[1:2, :]
    for peer in peers:
        pltpu.make_async_copy(gathered.at[peer], gathered.at[peer], stat_recv.at[peer]).wait()
        most = jnp.maximum(most, gathered[peer, 0:1, :])
        least = jnp.minimum(least, gathered[peer, 1:2, :])
    value_low[...] = least
    value_step[...] = (most - least) / 3.0
    for d in range(KV_HEADS - 1):
        pltpu.make_async_copy(stat, stat, stat_send.at[d]).wait()

    lax.fori_loop(STEPS - 1, STEPS, step, 0)
    past = held[...]
    for t in FULL_OUT[0]:
        weigh(t)
    for t in FULL_OUT[1]:
        gather(past, t)

    for here in range(XS):
        @pl.when(x == here)
        def _():
            for d in range(3):
                for row in range(REACH):
                    count = PLAN[here][3][d][row]
                    if count:
                        @pl.when(jnp.logical_and(z >= row, z < ZS - 1) if d == 2 else z >= row)
                        def _():
                            block = kv.at[pl.ds(0, count)]
                            pltpu.make_async_copy(block, block, send_sems.at[d, row]).wait()


def finish(acc, key_low, key_step, value_low, value_step, out_hbm, *rest):
    small, (out_v, sems) = rest[:4], rest[4:]
    copies = [
        pltpu.make_async_copy(src, dst, sems.at[i])
        for i, (src, dst) in enumerate(zip((key_low, key_step, value_low, value_step), small))
    ]
    for copy in copies:
        copy.start()
    for t in range(TILES):
        p, h = divmod(t, PER)
        part = acc[t, 0:HEAD_DIM] * (1.0 / acc[t, HEAD_DIM : HEAD_DIM + 1])
        out_v[pl.ds(p * TILE, TILE), pl.ds(h * HEAD_DIM, HEAD_DIM)] = part.astype(jnp.bfloat16).T
        if h == PER - 1:
            block = pl.ds(p * TILE, TILE)
            copies.append(pltpu.make_async_copy(out_v.at[block], out_hbm.at[block], sems.at[4 + p]))
            copies[-1].start()
    for copy in copies:
        copy.wait()


def shards(queries, new_keys, new_values):
    hbm = pl.BlockSpec(memory_space=pl.ANY)
    vmem = pl.BlockSpec(memory_space=pltpu.VMEM)
    f32, bf16 = jnp.float32, jnp.bfloat16
    chunks = TOK // CHUNK
    small = (
        ((chunks, HEAD_DIM), f32),
        ((chunks, HEAD_DIM), f32),
        ((1, TOK), f32),
        ((1, TOK), f32),
    )
    state = pl.pallas_call(
        kernel,
        out_shape=(pltpu.VMEM((TILES, DEEP, TILE), f32),) + tuple(pltpu.VMEM(*one) for one in small),
        in_specs=[hbm] * 3,
        out_specs=(vmem,) * 5,
        scratch_shapes=[
            pltpu.VMEM((OWN + 4, 2, CHUNK, HEAD_DIM), bf16),
            pltpu.VMEM((TOK, PER * HEAD_DIM), bf16),
            pltpu.VMEM((TILES, 2 * HEAD_DIM, TILE), bf16),
            pltpu.VMEM((TILES, 2 * CHUNK, TILE), f32),
            pltpu.VMEM((TILES, 2 * CHUNK, TILE), bf16),
            pltpu.VMEM((TILES, 1, TILE), f32),
            pltpu.VMEM((TILES, 1, TILE), f32),
            pltpu.VMEM((DEEP, 2 * CHUNK), bf16),
            pltpu.VMEM((2, TOK), f32),
            pltpu.VMEM((KV_HEADS, 2, TOK), f32),
            pltpu.SMEM((OPS,), jnp.int32),
            pltpu.SMEM((STEPS + 1,), jnp.int32),
            pltpu.SMEM((STEPS,), jnp.int32),
            pltpu.SemaphoreType.DMA((3,)),
            pltpu.SemaphoreType.DMA((OWN,)),
            pltpu.SemaphoreType.DMA((3, REACH)),
            pltpu.SemaphoreType.DMA((KV_HEADS - 1,)),
            pltpu.SemaphoreType.DMA((KV_HEADS,)),
        ],
        compiler_params=pltpu.CompilerParams(collective_id=0, has_side_effects=True),
    )(
        queries,
        new_keys.reshape(chunks, CHUNK, HEAD_DIM),
        new_values.reshape(chunks, CHUNK, HEAD_DIM),
    )
    state = [pltpu.with_memory_space_constraint(part, pltpu.VMEM) for part in state]
    attended, key_low, key_step, value_low, value_step = pl.pallas_call(
        finish,
        out_shape=(jax.ShapeDtypeStruct((TOK, PER * HEAD_DIM), bf16),)
        + tuple(jax.ShapeDtypeStruct(*one) for one in small),
        in_specs=[vmem] * 5,
        out_specs=(hbm,) * 5,
        scratch_shapes=[
            pltpu.VMEM((TOK, PER * HEAD_DIM), bf16),
            pltpu.SemaphoreType.DMA((4 + TOK // TILE,)),
        ],
    )(*state)
    return attended, key_low, key_step, value_low.reshape(TOK), value_step.reshape(TOK)


def solution(mesh):
    return jax.shard_map(
        shards,
        mesh=mesh,
        in_specs=(P("seq", "head"), P("seq", "head"), P("seq", "head")),
        out_specs=(P("seq", "head"), P("seq", "head"), P("seq", "head"), P("seq"), P("seq")),
        check_vma=False,
    )
```

time: 33.7 us -> 29.3 us (0.87); the launches traced: 33 us -> 29.2 us
  Pallas kernels: 32.4 us -> 28.6 us
    pallas_call x1, Pallas kernels: 30.9 us -> 27.6 us  [shards(): pl.pallas_call(kernel, out_shape=(pltpu.VMEM((TILES, DEEP, TILE), f32),)...]
    pallas_call x1, Pallas kernels: 1.53 us -> 0.98 us  [shards(): pl.pallas_call(finish, out_shape=(jax.ShapeDtypeStruct((TOK, PER * HEAD_D...]
where the time goes in v3:
time: 29.3 us; the launch traced here: 29.2 us
  Pallas kernels  28.6 us (98%)
  between operations  0.64 us (2%)
    pallas_call x1, Pallas kernels, shards(): pl.pallas_call(kernel, out_shape=(pltpu.VMEM((TILES, DEEP, TILE), f32),)...  27.6 us
    pallas_call x1, Pallas kernels, shards(): pl.pallas_call(finish, out_shape=(jax.ShapeDtypeStruct((TOK, PER * HEAD_D...  0.98 us

profile of v3, /device:TPU:160, one launch (start us, length us, event | category | flops | bytes accessed | tf_op | source)
XLA Modules:
  0.0 29.2 jit_solution(4335587068767407481)
XLA Ops:
  0.6 27.6 %shard_map.74 = (f32[8,144,256]{2,1,0:T(8,128)S(1)}, f32[4,128]{1,0:T(4,128)S(1)}, f32[4,128]{1,0:T(4,128)S(1)}, f32[1,512]{1,0:T(1,128)S(1)}, f32[1,512]{1,0:T(1,128)S(1)}) custom-call(bf16[512,512]{1,0:T(8,128)(2,1)} %q_hbm.1, bf16[4,128,128]{2,1,0:T(8,128)(2,1)} %bitcast.4, bf16[4,128,128]{2,1,0:T(8,128)(2,1)} %bitcast.5), custom_call_target="tpu_custom_call" | custom-call | tf_op jit(solution)/shard_map/pallas_call | solution.py:301
  28.2 1.0 %shard_map.75 = (bf16[512,512]{1,0:T(8,128)(2,1)}, f32[4,128]{1,0:T(4,128)}, f32[4,128]{1,0:T(4,128)}, f32[1,512]{1,0:T(1,128)}, f32[1,512]{1,0:T(1,128)}) custom-call(f32[8,144,256]{2,1,0:T(8,128)S(1)} %get-tuple-element.15.acc, f32[4,128]{1,0:T(4,128)S(1)} %get-tuple-element.16.key_low, f32[4,128]{1,0:T(4,128)S(1)} %get-tuple-element.17.key_step, ...), custom_call_target="tpu_custom_call" | custom-call | tf_op jit(solution)/shard_map/pallas_call | solution.py:333

commit v4 on v3

--- a/solution.py
+++ b/solution.py
@@ -29,32 +29,32 @@
 
 PLAN = (
     (
-        (34881, 18434, 2255, 34816, 2121, 18631, 18499, 35011, 53312, 34946, 18566, 4163, 20557, 36941, 53248, 4098, 20492, 36876, 53440, 4299, 20689, 37071, 53632, 53568, 4437, 53376, 4234, 20624, 37006, 54272, 53504, 2190, 4372, 58176, 53696, 20957, 37331, 53824, 58112, 58496, 53760, 4632, 37404, 58304, 53952, 21211, 37595, 53888, 37530, 58240, 54336, 58816, 58560, 54528, 38174, 54592, 59136, 10014, 58880, 58752, 59072, 58944, 59008, 59200, 59328, 59264),
-        (8, 18, 29, 33, 37, 43, 49, 50, 53, 55, 58, 60, 62, 63, 64, 66),
-        (1, 1, 1, 1, 1, 1, 2, 1, 2, 1, 2, 2, 2, 2, 2),
-        ((3, 7, 1), (4, 6, 0), (4, 9, 0)),
+        (18434, 18499, 34881, 34950, 2123, 2180, 34816, 53312, 4167, 20557, 36945, 53632, 2245, 18574, 37266, 53248, 35015, 4102, 20492, 36880, 53440, 18639, 20695, 58432, 2058, 53504, 4366, 53376, 20630, 37006, 58496, 53568, 4431, 53952, 53696, 37331, 53760, 54080, 21339, 58368, 53824, 4693, 37469, 53888, 21150, 37526, 58240, 9112, 54016, 37658, 58304, 58560, 58624, 9500, 54848, 38495, 59200, 58688, 58816, 58752, 54784, 59072, 59008, 59136, 59264, 59328),
+        (7, 20, 30, 33, 36, 43, 46, 50, 51, 54, 58, 60, 61, 63, 64, 66),
+        (1, 1, 1, 1, 1, 1, 1, 2, 2, 2, 2, 1, 2, 2, 2),
+        ((4, 5, 2), (4, 6, 0), (4, 9, 0)),
+        8,
+    ),
+    (
+        (2176, 35009, 34944, 34883, 34818, 2241, 49856, 53312, 2121, 4167, 20547, 36953, 49408, 33040, 53248, 4102, 20482, 53440, 2056, 4309, 20683, 37079, 53696, 54080, 21325, 53376, 20618, 37014, 49472, 337, 33105, 58944, 26191, 53760, 53632, 4498, 54272, 53824, 21081, 37459, 49792, 662, 58816, 26071, 54016, 54144, 58752, 59072, 26331, 54208, 5085, 37853, 54336, 5215, 58496, 25758, 54592, 38239, 58560, 54528, 58880, 59008, 59200, 59136, 59264, 59328),
+        (6, 17, 28, 31, 36, 40, 42, 45, 52, 56, 59, 60, 61, 63, 65, 66),
+        (1, 1, 0, 1, 1, 0, 1, 1, 1, 2, 1, 2, 2, 2, 2),
+        ((6, 6, 0), (0, 6, 4), (6, 6, 0)),
+        11,
+    ),
+    (
+        (2180, 2123, 35013, 34818, 34883, 2245, 49152, 34948, 8, 53568, 20813, 37199, 49216, 73, 53376, 2058, 4240, 20616, 37004, 53440, 4305, 20681, 37069, 49728, 601, 55040, 53504, 20748, 37134, 53696, 58304, 25563, 50624, 53632, 58112, 25362, 53888, 21140, 37528, 49664, 536, 33300, 58176, 53952, 37593, 54592, 5471, 58240, 25498, 54464, 50240, 58880, 26142, 50176, 33822, 54400, 54528, 59008, 50560, 58944, 59072, 55104, 55168, 55232),
+        (6, 14, 23, 29, 34, 42, 45, 49, 55, 56, 57, 59, 60, 61, 63, 64),
+        (0, 1, 1, 1, 0, 1, 2, 0, 1, 1, 0, 2, 2, 1, 1),
+        ((8, 3, 0), (0, 5, 4), (6, 6, 0)),
         6,
     ),
     (
-        (2241, 2176, 34944, 34820, 2117, 2052, 35009, 50112, 991, 53248, 4104, 20486, 36882, 49728, 34885, 53504, 4368, 20752, 37136, 53312, 20551, 36947, 53440, 53696, 58496, 25746, 53376, 4238, 54080, 21323, 37723, 53568, 4433, 20817, 37201, 53952, 53632, 20884, 37270, 58368, 25624, 54592, 5461, 38237, 49664, 58560, 53888, 54016, 59072, 9945, 50048, 926, 54848, 38495, 58432, 25689, 54528, 58816, 26079, 58752, 54784, 59008, 59200, 59136, 59328, 59264),
-        (7, 22, 28, 35, 39, 45, 47, 48, 52, 56, 57, 60, 61, 63, 64, 66),
-        (1, 1, 1, 1, 0, 1, 1, 0, 2, 1, 2, 1, 2, 2, 2),
-        ((6, 5, 1), (0, 6, 4), (4, 8, 0)),
-        8,
-    ),
-    (
-        (35011, 34887, 34946, 2068, 2249, 49216, 34822, 75, 32841, 53440, 2184, 20679, 37083, 49152, 10, 53696, 20941, 49472, 339, 53376, 4238, 20614, 37018, 49792, 17032, 49408, 274, 53632, 20876, 37272, 54528, 2133, 38162, 51136, 34775, 53824, 54080, 21337, 37725, 53760, 59072, 26327, 49856, 54272, 5150, 59008, 54016, 37660, 54144, 58880, 26138, 54208, 58496, 25756, 54336, 58560, 54720, 54592, 54656, 59200, 58944, 59136, 51072),
-        (5, 15, 23, 27, 30, 40, 43, 48, 52, 55, 56, 58, 59, 61, 63, 63),
-        (0, 1, 0, 1, 1, 0, 1, 1, 1, 2, 1, 1, 2, 2, 0),
-        ((8, 2, 0), (1, 5, 3), (6, 6, 0)),
-        12,
-    ),
-    (
-        (34881, 34816, 35013, 50432, 34948, 34074, 53312, 4165, 36951, 49280, 16522, 49728, 33359, 53248, 4100, 20500, 36886, 49600, 53568, 4425, 20813, 37209, 49344, 16587, 49856, 53504, 4360, 20748, 37144, 49536, 49664, 54912, 5770, 54080, 21327, 49792, 33436, 58816, 9687, 26067, 54016, 50368, 34015, 54208, 5077, 54336, 54144, 58752, 9622, 54272, 21526, 50304, 58944, 9821, 55104, 50496, 58880, 54976, 55168, 55040, 55232),
-        (3, 17, 24, 29, 31, 33, 37, 41, 47, 51, 52, 56, 57, 59, 60, 61),
-        (1, 0, 1, 0, 0, 0, 1, 1, 1, 0, 0, 2, 1, 1, 1),
-        ((0, 6, 3), (2, 5, 1), (8, 4, 0)),
-        11,
+        (34944, 35009, 34822, 49408, 34887, 33050, 53248, 4100, 20508, 36884, 49280, 49856, 53312, 4165, 36949, 49344, 16599, 49472, 53632, 4488, 20874, 37266, 49664, 53696, 4553, 20939, 37331, 54080, 21331, 54912, 5772, 49728, 50048, 17296, 33692, 58624, 9492, 25882, 49792, 54016, 58688, 9557, 25947, 54272, 5144, 50112, 33757, 54336, 58496, 9372, 54720, 50752, 58560, 54656, 55040, 50688, 54976, 55104, 55232, 55168),
+        (3, 15, 17, 22, 27, 32, 39, 40, 47, 48, 53, 54, 57, 57, 60, 60),
+        (1, 0, 0, 1, 0, 0, 1, 0, 1, 2, 1, 0, 1, 1, 1),
+        ((0, 6, 3), (2, 4, 2), (7, 4, 0)),
+        9,
     ),
 )
 OPS = max(len(plan[0]) for plan in PLAN)

time: 29.3 us -> 28.7 us (0.980)
  Pallas kernels: 28.6 us -> 28 us
    pallas_call x1, Pallas kernels: 27.6 us -> 27 us  [shards(): pl.pallas_call(kernel, out_shape=(pltpu.VMEM((TILES, DEEP, TILE), f32),)...]
where the time goes in v4:
time: 28.7 us; the launch traced here: 28.6 us
  Pallas kernels  28 us (98%)
  between operations  0.64 us (2%)
    pallas_call x1, Pallas kernels, shards(): pl.pallas_call(kernel, out_shape=(pltpu.VMEM((TILES, DEEP, TILE), f32),)...  27 us
    pallas_call x1, Pallas kernels, shards(): pl.pallas_call(finish, out_shape=(jax.ShapeDtypeStruct((TOK, PER * HEAD_D...  0.98 us

profile of v4, /device:TPU:160, one launch (start us, length us, event | category | flops | bytes accessed | tf_op | source)
XLA Modules:
  0.0 28.6 jit_solution(17313635146092894765)
XLA Ops:
  0.6 27.0 %shard_map.74 = (f32[8,144,256]{2,1,0:T(8,128)S(1)}, f32[4,128]{1,0:T(4,128)S(1)}, f32[4,128]{1,0:T(4,128)S(1)}, f32[1,512]{1,0:T(1,128)S(1)}, f32[1,512]{1,0:T(1,128)S(1)}) custom-call(bf16[512,512]{1,0:T(8,128)(2,1)} %q_hbm.1, bf16[4,128,128]{2,1,0:T(8,128)(2,1)} %bitcast.4, bf16[4,128,128]{2,1,0:T(8,128)(2,1)} %bitcast.5), custom_call_target="tpu_custom_call" | custom-call | tf_op jit(solution)/shard_map/pallas_call | solution.py:301
  27.7 1.0 %shard_map.75 = (bf16[512,512]{1,0:T(8,128)(2,1)}, f32[4,128]{1,0:T(4,128)}, f32[4,128]{1,0:T(4,128)}, f32[1,512]{1,0:T(1,128)}, f32[1,512]{1,0:T(1,128)}) custom-call(f32[8,144,256]{2,1,0:T(8,128)S(1)} %get-tuple-element.15.acc, f32[4,128]{1,0:T(4,128)S(1)} %get-tuple-element.16.key_low, f32[4,128]{1,0:T(4,128)S(1)} %get-tuple-element.17.key_step, ...), custom_call_target="tpu_custom_call" | custom-call | tf_op jit(solution)/shard_map/pallas_call | solution.py:333

commit v5 on v3

--- a/solution.py
+++ b/solution.py
@@ -29,32 +29,32 @@
 
 PLAN = (
     (
-        (34881, 18434, 2255, 34816, 2121, 18631, 18499, 35011, 53312, 34946, 18566, 4163, 20557, 36941, 53248, 4098, 20492, 36876, 53440, 4299, 20689, 37071, 53632, 53568, 4437, 53376, 4234, 20624, 37006, 54272, 53504, 2190, 4372, 58176, 53696, 20957, 37331, 53824, 58112, 58496, 53760, 4632, 37404, 58304, 53952, 21211, 37595, 53888, 37530, 58240, 54336, 58816, 58560, 54528, 38174, 54592, 59136, 10014, 58880, 58752, 59072, 58944, 59008, 59200, 59328, 59264),
-        (8, 18, 29, 33, 37, 43, 49, 50, 53, 55, 58, 60, 62, 63, 64, 66),
-        (1, 1, 1, 1, 1, 1, 2, 1, 2, 1, 2, 2, 2, 2, 2),
-        ((3, 7, 1), (4, 6, 0), (4, 9, 0)),
+        (2052, 34881, 34816, 18633, 18434, 18499, 34946, 53312, 35011, 4169, 20557, 36941, 53248, 18568, 2117, 20492, 36876, 53376, 2188, 20628, 37006, 53504, 20760, 53440, 20693, 37071, 53632, 4494, 53568, 20825, 37203, 58176, 53696, 4559, 37333, 53760, 58112, 53952, 4819, 53824, 21087, 37465, 58240, 53888, 4754, 58304, 54336, 37979, 54272, 58560, 9433, 58496, 58624, 58688, 9565, 54720, 38367, 54656, 58944, 58880, 59200, 59072, 59008, 59136, 59328, 59264),
+        (7, 17, 26, 31, 35, 42, 45, 48, 51, 53, 57, 58, 60, 63, 64, 66),
+        (1, 1, 1, 1, 1, 1, 2, 1, 2, 2, 1, 2, 2, 2, 2),
+        ((3, 5, 2), (4, 7, 0), (4, 9, 0)),
         6,
     ),
     (
-        (2241, 2176, 34944, 34820, 2117, 2052, 35009, 50112, 991, 53248, 4104, 20486, 36882, 49728, 34885, 53504, 4368, 20752, 37136, 53312, 20551, 36947, 53440, 53696, 58496, 25746, 53376, 4238, 54080, 21323, 37723, 53568, 4433, 20817, 37201, 53952, 53632, 20884, 37270, 58368, 25624, 54592, 5461, 38237, 49664, 58560, 53888, 54016, 59072, 9945, 50048, 926, 54848, 38495, 58432, 25689, 54528, 58816, 26079, 58752, 54784, 59008, 59200, 59136, 59328, 59264),
-        (7, 22, 28, 35, 39, 45, 47, 48, 52, 56, 57, 60, 61, 63, 64, 66),
-        (1, 1, 1, 1, 0, 1, 1, 0, 2, 1, 2, 1, 2, 2, 2),
-        ((6, 5, 1), (0, 6, 4), (4, 8, 0)),
-        8,
-    ),
-    (
-        (35011, 34887, 34946, 2068, 2249, 49216, 34822, 75, 32841, 53440, 2184, 20679, 37083, 49152, 10, 53696, 20941, 49472, 339, 53376, 4238, 20614, 37018, 49792, 17032, 49408, 274, 53632, 20876, 37272, 54528, 2133, 38162, 51136, 34775, 53824, 54080, 21337, 37725, 53760, 59072, 26327, 49856, 54272, 5150, 59008, 54016, 37660, 54144, 58880, 26138, 54208, 58496, 25756, 54336, 58560, 54720, 54592, 54656, 59200, 58944, 59136, 51072),
-        (5, 15, 23, 27, 30, 40, 43, 48, 52, 55, 56, 58, 59, 61, 63, 63),
-        (0, 1, 0, 1, 1, 0, 1, 1, 1, 2, 1, 1, 2, 2, 0),
-        ((8, 2, 0), (1, 5, 3), (6, 6, 0)),
+        (34816, 34881, 34946, 2184, 49408, 2117, 35011, 278, 33032, 53248, 20484, 36888, 53312, 2052, 2249, 4181, 20549, 53376, 4242, 20616, 37018, 53824, 53632, 37264, 53440, 4307, 20681, 37083, 49472, 343, 53696, 20945, 53760, 49920, 794, 33556, 53888, 58880, 26130, 53952, 21207, 59008, 26264, 54144, 49984, 33621, 58368, 25626, 54208, 59072, 58432, 54464, 38111, 54528, 5406, 58752, 26014, 54400, 38046, 54592, 58816, 58944, 59328, 59136, 59200, 59264),
+        (4, 17, 28, 30, 33, 39, 41, 46, 49, 51, 59, 60, 61, 62, 65, 66),
+        (1, 1, 0, 1, 1, 1, 0, 1, 2, 1, 1, 2, 2, 2, 2),
+        ((7, 4, 0), (0, 6, 4), (7, 6, 0)),
         12,
     ),
     (
-        (34881, 34816, 35013, 50432, 34948, 34074, 53312, 4165, 36951, 49280, 16522, 49728, 33359, 53248, 4100, 20500, 36886, 49600, 53568, 4425, 20813, 37209, 49344, 16587, 49856, 53504, 4360, 20748, 37144, 49536, 49664, 54912, 5770, 54080, 21327, 49792, 33436, 58816, 9687, 26067, 54016, 50368, 34015, 54208, 5077, 54336, 54144, 58752, 9622, 54272, 21526, 50304, 58944, 9821, 55104, 50496, 58880, 54976, 55168, 55040, 55232),
-        (3, 17, 24, 29, 31, 33, 37, 41, 47, 51, 52, 56, 57, 59, 60, 61),
-        (1, 0, 1, 0, 0, 0, 1, 1, 1, 0, 0, 2, 1, 1, 1),
-        ((0, 6, 3), (2, 5, 1), (8, 4, 0)),
-        11,
+        (34944, 2182, 35009, 34818, 2062, 49664, 540, 53248, 34883, 2247, 20486, 36878, 53312, 4171, 20551, 36943, 53376, 4250, 20618, 37004, 49472, 2127, 343, 53632, 53440, 20683, 37069, 50560, 34192, 50880, 18125, 58240, 49408, 278, 33044, 53696, 58304, 25553, 49728, 605, 53952, 58112, 25366, 54592, 53888, 37532, 58176, 25431, 54400, 5278, 54336, 54272, 54464, 58880, 26140, 54528, 50624, 58944, 59136, 50816, 59200, 55168, 55232),
+        (5, 16, 27, 35, 38, 43, 46, 48, 52, 55, 56, 59, 59, 61, 62, 63),
+        (1, 1, 0, 1, 0, 1, 2, 1, 1, 1, 0, 2, 0, 2, 1),
+        ((8, 3, 0), (1, 4, 4), (6, 5, 0)),
+        6,
+    ),
+    (
+        (34816, 34881, 35013, 49536, 34948, 33162, 53248, 4102, 20486, 36880, 49728, 16987, 50048, 53312, 4167, 20551, 36945, 49280, 53568, 4427, 20811, 37203, 49344, 50944, 53504, 4362, 20746, 37138, 54080, 21329, 49600, 53888, 4752, 49664, 53952, 58368, 9236, 25624, 54016, 54912, 5782, 58432, 25689, 54528, 50112, 33755, 58560, 9437, 25821, 54784, 50624, 58496, 9372, 54592, 21855, 50560, 54848, 54976, 51008, 55232, 55168),
+        (3, 17, 23, 28, 31, 34, 35, 39, 46, 53, 56, 57, 59, 60, 61, 61),
+        (1, 0, 1, 0, 0, 1, 1, 0, 2, 1, 0, 1, 1, 0, 1),
+        ((0, 6, 3), (1, 6, 3), (6, 4, 0)),
+        8,
     ),
 )
 OPS = max(len(plan[0]) for plan in PLAN)
@@ -279,9 +279,9 @@
         p, h = divmod(t, PER)
         part = acc[t, 0:HEAD_DIM] * (1.0 / acc[t, HEAD_DIM : HEAD_DIM + 1])
         out_v[pl.ds(p * TILE, TILE), pl.ds(h * HEAD_DIM, HEAD_DIM)] = part.astype(jnp.bfloat16).T
-        if h == PER - 1:
-            block = pl.ds(p * TILE, TILE)
-            copies.append(pltpu.make_async_copy(out_v.at[block], out_hbm.at[block], sems.at[4 + p]))
+        if h % 2 == 1:
+            block = (pl.ds(p * TILE, TILE), pl.ds((h - 1) * HEAD_DIM, 2 * HEAD_DIM))
+            copies.append(pltpu.make_async_copy(out_v.at[block], out_hbm.at[block], sems.at[4 + t // 2]))
             copies[-1].start()
     for copy in copies:
         copy.wait()
@@ -338,7 +338,7 @@
         out_specs=(hbm,) * 5,
         scratch_shapes=[
             pltpu.VMEM((TOK, PER * HEAD_DIM), bf16),
-            pltpu.SemaphoreType.DMA((4 + TOK // TILE,)),
+            pltpu.SemaphoreType.DMA((4 + TILES // 2,)),
         ],
     )(*state)
     return attended, key_low, key_step, value_low.reshape(TOK), value_step.reshape(TOK)

time: 29.3 us -> 28.4 us (0.969)
  Pallas kernels: 28.6 us -> 27.6 us
    pallas_call x1, Pallas kernels: 27.6 us -> 26.7 us  [shards(): pl.pallas_call(kernel, out_shape=(pltpu.VMEM((TILES, DEEP, TILE), f32),)...]
where the time goes in v5:
time: 28.4 us; the launch traced here: 28.3 us
  Pallas kernels  27.6 us (97%)
  between operations  0.64 us (2%)
    pallas_call x1, Pallas kernels, shards(): pl.pallas_call(kernel, out_shape=(pltpu.VMEM((TILES, DEEP, TILE), f32),)...  26.7 us
    pallas_call x1, Pallas kernels, shards(): pl.pallas_call(finish, out_shape=(jax.ShapeDtypeStruct((TOK, PER * HEAD_D...  0.96 us

profile of v5, /device:TPU:160, one launch (start us, length us, event | category | flops | bytes accessed | tf_op | source)
XLA Modules:
  0.0 28.3 jit_solution(3320212853180550210)
XLA Ops:
  0.6 26.7 %shard_map.74 = (f32[8,144,256]{2,1,0:T(8,128)S(1)}, f32[4,128]{1,0:T(4,128)S(1)}, f32[4,128]{1,0:T(4,128)S(1)}, f32[1,512]{1,0:T(1,128)S(1)}, f32[1,512]{1,0:T(1,128)S(1)}) custom-call(bf16[512,512]{1,0:T(8,128)(2,1)} %q_hbm.1, bf16[4,128,128]{2,1,0:T(8,128)(2,1)} %bitcast.4, bf16[4,128,128]{2,1,0:T(8,128)(2,1)} %bitcast.5), custom_call_target="tpu_custom_call" | custom-call | tf_op jit(solution)/shard_map/pallas_call | solution.py:301
  27.3 1.0 %shard_map.75 = (bf16[512,512]{1,0:T(8,128)(2,1)}, f32[4,128]{1,0:T(4,128)}, f32[4,128]{1,0:T(4,128)}, f32[1,512]{1,0:T(1,128)}, f32[1,512]{1,0:T(1,128)}) custom-call(f32[8,144,256]{2,1,0:T(8,128)S(1)} %get-tuple-element.15.acc, f32[4,128]{1,0:T(4,128)S(1)} %get-tuple-element.16.key_low, f32[4,128]{1,0:T(4,128)S(1)} %get-tuple-element.17.key_step, ...), custom_call_target="tpu_custom_call" | custom-call | tf_op jit(solution)/shard_map/pallas_call | solution.py:333
